TPU v7x, 512 devices: a whole 4x8x8 slice. The times are simulated.
512 devices in a mesh: mem: 16 (over z, core), tile: 32 (over y, x).
Axes of the slice: x: 4, y: 8, z: 8, core: 2. Of those that a mesh axis runs over, the one named last changes fastest.
Arguments:
- ensemble: float32 [512, 4, 1024, 128], P('mem', None, 'tile'), may hold values from -16 to 16
- diffusion: float32 [4, 1024, 128], P(None, 'tile'), may hold values from 0.04 to 0.12
- obs_cells: int32 [32, 16, 512], P('tile', 'mem'), may hold values from 0 to 3071
- obs_values: float32 [32, 16, 512], P('tile', 'mem'), may hold values from -6 to 6
- obs_weights: float32 [32, 16, 512], P('tile', 'mem'), may hold values from 12 to 36
Outputs:
- analysis: float32 [512, 4, 1024, 128], P('mem', None, 'tile')
Inputs may be any that keep to these rules, and one draw needn't show every extreme that they name: `obs_cells`: index e below 1024 is cell e of the patch before (mem index minus one, cyclically, same tile); then come the patch's own 1024 cells, then those of the patch after.
All inputs are finite; a program needn't handle non-finite values.
Results may differ from a plain program's by a relative error of at most 0.019.
The roundings to bfloat16 on the way count: a program that leaves them out, or rounds other values in their place, can miss the bound.
Values may be sent and summed in bfloat16 or wider, within the bound.
A program may use at most 64 MiB of HBM per device.

v0:
```python
import jax
import jax.numpy as jnp
from jax import lax
from jax.sharding import PartitionSpec as P

ITERS = 6
SUB = 3


advect = 0.3
vertical = 0.1


def with_halo(value, sides, width, wrap):
    for axis, dim in sides:
        size, length = (lax.axis_size(axis), value.shape[dim])
        up = [(i, (i + 1) % size) for i in range(size if wrap else size - 1)]
        down = [(j, i) for i, j in up]
        last = lax.slice_in_dim(value, length - width, length, axis=dim)
        initial = lax.slice_in_dim(value, 0, width, axis=dim)
        before = lax.ppermute(last, axis, up)
        after = lax.ppermute(initial, axis, down)
        value = jnp.concatenate([before, value, after], axis=dim)
    return value


def stencil(padded, diffusion):
    extended = jnp.pad(padded, ((0, 0), (1, 1), (0, 0), (1, 1)))
    centre = extended[:, 1:-1, 1:-1, 1:-1]
    west_side = extended[:, 1:-1, :-2, 1:-1]
    east_side = extended[:, 1:-1, 2:, 1:-1]
    south_side = extended[:, 1:-1, 1:-1, :-2]
    north_side = extended[:, 1:-1, 1:-1, 2:]
    level_above = extended[:, 2:, 1:-1, 1:-1]
    level_below = extended[:, :-2, 1:-1, 1:-1]
    laplace = west_side + east_side + south_side + north_side - 4.0 * centre
    return (
        centre
        + diffusion * laplace
        + advect * (west_side - centre)
        + vertical * (level_above + level_below - 2.0 * centre)
    )


def analyse(cellwise, predicted, values, weights):
    members = cellwise.shape[0]
    identity = jnp.eye(members, dtype=jnp.float32)
    pfloat = predicted.astype(jnp.float32)
    pmean = jnp.mean(pfloat, axis=0)
    ppert = pfloat - pmean
    innov = values - pmean
    left = (ppert * weights).astype(jnp.bfloat16)
    right = ppert.astype(jnp.bfloat16)
    gram = lax.dot_general(
        left, right, (((1,), (1,)), ((), ())), preferred_element_type=jnp.float32
    )
    cov = identity + gram / (members - 1.0)
    scale = 3.0 * jnp.trace(cov) / members
    yiter = cov / scale
    ziter = identity
    for repeat in range(ITERS):
        middle = 1.5 * identity - 0.5 * jnp.dot(
            ziter.astype(jnp.bfloat16),
            yiter.astype(jnp.bfloat16),
            preferred_element_type=jnp.float32,
        )
        mbf = middle.astype(jnp.bfloat16)
        yiter = jnp.dot(yiter.astype(jnp.bfloat16), mbf, preferred_element_type=jnp.float32)
        ziter = jnp.dot(mbf, ziter.astype(jnp.bfloat16), preferred_element_type=jnp.float32)
    root = ziter / jnp.sqrt(scale)
    drive = jnp.dot(ppert, weights * innov, precision=lax.Precision.HIGHEST) / (members - 1.0)
    wmean = jnp.dot(
        root, jnp.dot(root, drive, precision=lax.Precision.HIGHEST), precision=lax.Precision.HIGHEST
    )
    wtotal = (root + wmean[:, None]).astype(jnp.bfloat16)
    cfloat = cellwise.astype(jnp.float32)
    xmean = jnp.mean(cfloat, axis=0)
    xpert = (cfloat - xmean).astype(jnp.bfloat16)
    update = lax.dot_general(
        wtotal, xpert, (((0,), (0,)), ((), ())), preferred_element_type=jnp.float32
    )
    return xmean + update


def on_device(ensemble, diffusion, obs_cells, obs_values, obs_weights):
    local_members, levels, width, columns = ensemble.shape
    states = with_halo(ensemble, (("tile", 2),), SUB, False)
    wide_diff = with_halo(diffusion, (("tile", 1),), SUB, False)
    anchor = lax.axis_index("tile") * width
    total_width = width * lax.axis_size("tile")
    for repeat in range(SUB):
        margin = SUB - repeat - 1
        states = stencil(states, wide_diff[:, repeat + 1 : wide_diff.shape[1] - repeat - 1])
        positions = anchor - margin + lax.iota(jnp.int32, states.shape[2])
        inside = ((positions >= 0) & (positions < total_width)).astype(jnp.float32)
        states = states * inside[None, None, :, None]
    tile_cells = levels * width * columns
    shares = lax.axis_size("mem")
    patch_cells = tile_cells // shares
    background = states.astype(jnp.bfloat16).reshape(local_members, tile_cells)
    own_cells = obs_cells.reshape(-1)
    own_values = obs_values.reshape(-1)
    own_weights = obs_weights.reshape(-1)
    cellwise = lax.all_to_all(background, "mem", split_axis=1, concat_axis=0, tiled=True)
    extended = with_halo(cellwise, (("mem", 1),), patch_cells, True)
    predicted = jnp.take(extended, own_cells, axis=1)
    updated = analyse(cellwise, predicted, own_values, own_weights)
    returned = lax.all_to_all(updated, "mem", split_axis=0, concat_axis=1, tiled=True)
    return returned.reshape(local_members, levels, width, columns)


def solution(mesh):
    return jax.shard_map(
        on_device,
        mesh=mesh,
        in_specs=(
            P("mem", None, "tile", None),
            P(None, "tile", None),
            P("tile", "mem", None),
            P("tile", "mem", None),
            P("tile", "mem", None),
        ),
        out_specs=P("mem", None, "tile", None),
        check_vma=False,
    )
```

profile of v0, /device:TPU:31, one launch (start us, length us, event | category | flops | bytes accessed | tf_op | source)
XLA Modules:
  0.0 173.6 jit_solution(8284966104410556885)
XLA Ops:
  0.7 4.3 %collective-permute-start.2 = (f32[4,3,128]{2,1,0:T(4,128)S(1)}, f32[4,3,128]{2,1,0:T(4,128)S(1)}, u32[]{:S(2)}, u32[]{:S(2)}) collective-permute-start(f32[4,3,128]{2,1,0:T(4,128)S(1)} %get-tuple-element.7), channel_id=1, source_target_pairs={{0,1},{1,2},{2,3},{3,4},{4,5},{5,6},{6,7},{7,8},{8,9},{9,10},{10,1... | collective-permute-start | bytes 18440 | tf_op jit(solution)/shard_map/ppermute | solution.py:21
  5.1 1.9 %collective-permute-start.3 = (f32[4,3,128]{2,1,0:T(4,128)S(1)}, f32[4,3,128]{2,1,0:T(4,128)S(1)}, u32[]{:S(2)}, u32[]{:S(2)}) collective-permute-start(f32[4,3,128]{2,1,0:T(4,128)S(1)} %get-tuple-element.8), channel_id=1, source_target_pairs={{1,0},{2,1},{3,2},{4,3},{5,4},{6,5},{7,6},{8,7},{9,8},{10,9},{11,1... | collective-permute-start | bytes 18440 | tf_op jit(solution)/shard_map/ppermute | solution.py:22
  7.0 1.3 fusion.53
  8.3 6.7 %collective-permute-start = (f32[32,4,3,128]{3,2,1,0:T(4,128)S(1)}, f32[32,4,3,128]{3,2,1,0:T(4,128)S(1)}, u32[]{:S(2)}, u32[]{:S(2)}) collective-permute-start(f32[32,4,3,128]{3,2,1,0:T(4,128)S(1)} %get-tuple-element.5), channel_id=1, source_target_pairs={{0,1},{1,2},{2,3},{3,4},{4,5},{5,6},{6,7},{7,8},{8,9},{9,10},{10,1... | collective-permute-start | bytes 589832 | tf_op jit(solution)/shard_map/ppermute | solution.py:21
  15.0 1.9 %collective-permute-start.1 = (f32[32,4,3,128]{3,2,1,0:T(4,128)S(1)}, f32[32,4,3,128]{3,2,1,0:T(4,128)S(1)}, u32[]{:S(2)}, u32[]{:S(2)}) collective-permute-start(f32[32,4,3,128]{3,2,1,0:T(4,128)S(1)} %get-tuple-element.6), channel_id=1, source_target_pairs={{1,0},{2,1},{3,2},{4,3},{5,4},{6,5},{7,6},{8,7},{9,8},{10,9},{11,1... | collective-permute-start | bytes 589832 | tf_op jit(solution)/shard_map/ppermute | solution.py:22
  17.9 1.5 collective-permute-done
  19.4 7.2 %collective-permute-done.1 = f32[32,4,3,128]{3,2,1,0:T(4,128)S(1)} collective-permute-done((f32[32,4,3,128]{3,2,1,0:T(4,128)S(1)}, f32[32,4,3,128]{3,2,1,0:T(4,128)S(1)}, u32[]{:S(2)}, u32[]{:S(2)}) %collective-permute-start.1) | collective-permute-done | bytes 196640 | tf_op jit(solution)/shard_map/ppermute | solution.py:22
  26.6 1.9 %pad_maximum_fusion.1 = f32[32,4,38,128]{3,2,1,0:T(8,128)S(1)} fusion(f32[32,4,3,128]{3,2,1,0:T(4,128)S(1)} %collective-permute-done.1, f32[32,4,32,128]{3,2,1,0:T(8,128)} %param.5, f32[32,4,3,128]{3,2,1,0:T(4,128)S(1)} %collective-permute-done), kind=kLoop, calls=%fused_computation.44 | loop fusion | flops 1245184 | bytes 4980736 | tf_op jit(solution)/shard_map/concatenate | solution.py:23
  28.5 2.6 %fusion.7 = f32[32,4,36,128]{3,2,1,0:T(8,128)S(1)} fusion(f32[32,4,38,128]{3,2,1,0:T(8,128)S(1)} %pad_maximum_fusion.1, f32[36]{0:T(128)S(1)} %and_convert_fusion.2, f32[4,36,128]{2,1,0:T(8,128)S(1)} %slice.120), kind=kLoop, calls=%fused_computation.27 | loop fusion | flops 9437184 | bytes 12927488 | tf_op jit(solution)/shard_map/mul | solution.py:96
  31.2 2.6 %fusion.18 = f32[32,4,34,128]{3,2,1,0:T(8,128)S(1)} fusion(f32[32,4,36,128]{3,2,1,0:T(8,128)S(1)} %fusion.7, f32[34]{0:T(128)S(1)} %and_convert_fusion.1, f32[4,34,128]{2,1,0:T(8,128)S(1)} %slice.124), kind=kLoop, calls=%fused_computation.38 | loop fusion | flops 8912896 | bytes 12796416 | tf_op jit(solution)/shard_map/mul | solution.py:96
  33.8 2.2 %fusion.33 = bf16[32,4,32,128]{3,2,1,0:T(8,128)(2,1)S(1)} fusion(f32[32,4,34,128]{3,2,1,0:T(8,128)S(1)} %fusion.18, f32[32]{0:T(128)S(1)} %and_convert_fusion, f32[4,32,128]{2,1,0:T(8,128)S(1)} %copy-done.3), kind=kLoop, calls=%fused_computation.59 | loop fusion | flops 8912896 | bytes 10027520 | tf_op jit(solution)/shard_map/convert_element_type | solution.py:100
  37.1 40.9 %all_to_all.35 = bf16[32,16,1024]{2,0,1:T(8,128)(2,1)S(1)} all-to-all(bf16[32,16,1024]{2,0,1:T(8,128)(2,1)S(1)} %copy.9), channel_id=1, replica_groups=mesh['mem'=16,'tile'=32] {'mem'}, dimensions={1} | all-to-all | bytes 2097152 | tf_op jit(solution)/shard_map/all_to_all | solution.py:104
  78.8 11.0 %collective-permute-done.4 = bf16[512,1024]{1,0:T(8,128)(2,1)S(1)} collective-permute-done((bf16[512,1024]{1,0:T(8,128)(2,1)S(1)}, bf16[512,1024]{1,0:T(8,128)(2,1)S(1)}, u32[]{:S(2)}, u32[]{:S(2)}) %collective-permute-start.4) | collective-permute-done | bytes 1048608 | tf_op jit(solution)/shard_map/ppermute | solution.py:21
  89.8 2.5 %collective-permute-done.5 = bf16[512,1024]{1,0:T(8,128)(2,1)S(1)} collective-permute-done((bf16[512,1024]{1,0:T(8,128)(2,1)S(1)}, bf16[512,1024]{1,0:T(8,128)(2,1)S(1)}, u32[]{:S(2)}, u32[]{:S(2)}) %collective-permute-start.5) | collective-permute-done | bytes 1048608 | tf_op jit(solution)/shard_map/ppermute | solution.py:22
  92.3 1.7 %pad_maximum_fusion = bf16[512,3072]{1,0:T(8,128)(2,1)} fusion(bf16[512,1024]{1,0:T(8,128)(2,1)S(1)} %collective-permute-done.5, bf16[512,1024]{1,0:T(8,128)(2,1)S(1)} %bitcast.72, bf16[512,1024]{1,0:T(8,128)(2,1)S(1)} %collective-permute-done.4), kind=kLoop, calls=%fused_computation.13 | loop fusion | flops 9437184 | bytes 6291456 | tf_op jit(solution)/shard_map/concatenate | solution.py:23
  94.1 3.2 %copy.10 = bf16[512,3072]{0,1:T(8,128)(2,1)S(1)} copy(bf16[512,3072]{1,0:T(8,128)(2,1)} %pad_maximum_fusion) | data formatting | bytes 6291456 | tf_op jit(solution)/shard_map/concatenate | solution.py:23
  97.3 2.6 %gather_fusion = bf16[512,512]{1,0:T(8,128)(2,1)} fusion(bf16[512,3072]{0,1:T(8,128)(2,1)S(1)} %copy.10, s32[1024]{0:T(1024)S(1)} %pad_clamp_fusion), kind=kCustom, calls=%fused_computation | custom fusion | bytes 1050624 | tf_op jit(solution)/shard_map/jit(_take)/gather | solution.py:106
  99.9 1.3 convert_reduce_fusion.1
  101.2 2.7 %select_reduce_fusion = (f32[]{:T(128)}, f32[512,512]{1,0:T(8,128)S(1)}) fusion(f32[512]{0:T(512)S(1)} %get-tuple-element.10, bf16[512,512]{1,0:T(8,128)(2,1)} %gather_fusion, pred[512]{0:T(512)(128)(4,1)S(1)} %compare_and_fusion, f32[512]{0:T(512)S(1)} %bitcast.82), kind=kOutput, calls=%fused_computation.97 | convolution fusion | flops 272367616 | bytes 1577476 | tf_op jit(solution)/shard_map/dot_general | solution.py:54
  112.9 1.0 convolution_bitcast_fusion
  113.9 1.0 fusion.55
  115.8 55.2 %all_to_all.36 = f32[16,32,1024]{2,1,0:T(8,128)S(1)} all-to-all(f32[16,32,1024]{2,1,0:T(8,128)S(1)} %bitcast.75), channel_id=1, replica_groups=mesh['mem'=16,'tile'=32] {'mem'}, dimensions={0} | all-to-all | bytes 4194304 | tf_op jit(solution)/shard_map/all_to_all | solution.py:108
  170.9 1.2 copy.11
  172.2 1.5 reshape.93
  (52 shorter events, 12.5 us)
Async XLA Ops:
  0.7 16.3 %collective-permute-start.2 = (f32[4,3,128]{2,1,0:T(4,128)S(1)}, f32[4,3,128]{2,1,0:T(4,128)S(1)}, u32[]{:S(2)}, u32[]{:S(2)}) collective-permute-start(f32[4,3,128]{2,1,0:T(4,128)S(1)} %get-tuple-element.7), channel_id=1, source_target_pairs={{0,1},{1,2},{2,3},{3,4},{4,5},{5,6},{6,7},{7,8},{8,9},{9,10},{10,1... | collective-permute-start | bytes 18440 | tf_op jit(solution)/shard_map/ppermute | solution.py:21
  5.1 11.9 %collective-permute-start.3 = (f32[4,3,128]{2,1,0:T(4,128)S(1)}, f32[4,3,128]{2,1,0:T(4,128)S(1)}, u32[]{:S(2)}, u32[]{:S(2)}) collective-permute-start(f32[4,3,128]{2,1,0:T(4,128)S(1)} %get-tuple-element.8), channel_id=1, source_target_pairs={{1,0},{2,1},{3,2},{4,3},{5,4},{6,5},{7,6},{8,7},{9,8},{10,9},{11,1... | collective-permute-start | bytes 18440 | tf_op jit(solution)/shard_map/ppermute | solution.py:22
  8.3 11.1 %collective-permute-start = (f32[32,4,3,128]{3,2,1,0:T(4,128)S(1)}, f32[32,4,3,128]{3,2,1,0:T(4,128)S(1)}, u32[]{:S(2)}, u32[]{:S(2)}) collective-permute-start(f32[32,4,3,128]{3,2,1,0:T(4,128)S(1)} %get-tuple-element.5), channel_id=1, source_target_pairs={{0,1},{1,2},{2,3},{3,4},{4,5},{5,6},{6,7},{7,8},{8,9},{9,10},{10,1... | collective-permute-start | bytes 589832 | tf_op jit(solution)/shard_map/ppermute | solution.py:21
  15.0 11.6 %collective-permute-start.1 = (f32[32,4,3,128]{3,2,1,0:T(4,128)S(1)}, f32[32,4,3,128]{3,2,1,0:T(4,128)S(1)}, u32[]{:S(2)}, u32[]{:S(2)}) collective-permute-start(f32[32,4,3,128]{3,2,1,0:T(4,128)S(1)} %get-tuple-element.6), channel_id=1, source_target_pairs={{1,0},{2,1},{3,2},{4,3},{5,4},{6,5},{7,6},{8,7},{9,8},{10,9},{11,1... | collective-permute-start | bytes 589832 | tf_op jit(solution)/shard_map/ppermute | solution.py:22
  31.2 2.7 %copy-start.3 = (f32[4,32,128]{2,1,0:T(8,128)S(1)}, f32[4,32,128]{2,1,0:T(8,128)}, u32[]{:S(2)}) copy-start(f32[4,32,128]{2,1,0:T(8,128)} %param.6) | copy-start | bytes 196612
  36.5 42.1 %copy-start.4 = (s32[1,1,512]{2,1,0:T(1,128)S(1)}, s32[1,1,512]{2,1,0:T(1,128)}, u32[]{:S(2)}) copy-start(s32[1,1,512]{2,1,0:T(1,128)} %param.7) | copy-start | bytes 6148
  78.1 14.2 %copy-start = (bf16[32,16,1024]{2,0,1:T(8,128)(2,1)}, bf16[32,16,1024]{2,0,1:T(8,128)(2,1)S(1)}, u32[]{:S(2)}) copy-start(bf16[32,16,1024]{2,0,1:T(8,128)(2,1)S(1)} %all_to_all.35) | copy-start | bytes 3145732
  78.1 11.7 %collective-permute-start.4 = (bf16[512,1024]{1,0:T(8,128)(2,1)S(1)}, bf16[512,1024]{1,0:T(8,128)(2,1)S(1)}, u32[]{:S(2)}, u32[]{:S(2)}) collective-permute-start(bf16[512,1024]{1,0:T(8,128)(2,1)S(1)} %bitcast.70), channel_id=1, source_target_pairs={{0,32},{32,64},{64,96},{96,128},{128,160},{160,192},{192,224},{224... | collective-permute-start | bytes 3145736 | tf_op jit(solution)/shard_map/ppermute | solution.py:21
  78.1 14.2 %collective-permute-start.5 = (bf16[512,1024]{1,0:T(8,128)(2,1)S(1)}, bf16[512,1024]{1,0:T(8,128)(2,1)S(1)}, u32[]{:S(2)}, u32[]{:S(2)}) collective-permute-start(bf16[512,1024]{1,0:T(8,128)(2,1)S(1)} %bitcast.71), channel_id=1, source_target_pairs={{32,0},{64,32},{96,64},{128,96},{160,128},{192,160},{224,192},{256... | collective-permute-start | bytes 3145736 | tf_op jit(solution)/shard_map/ppermute | solution.py:22
  97.2 4.0 %copy-start.5 = (f32[1,1,512]{2,1,0:T(1,128)S(1)}, f32[1,1,512]{2,1,0:T(1,128)}, u32[]{:S(2)}) copy-start(f32[1,1,512]{2,1,0:T(1,128)} %param.8) | copy-start | bytes 6148
  97.3 4.0 %copy-start.6 = (f32[1,1,512]{2,1,0:T(1,128)S(1)}, f32[1,1,512]{2,1,0:T(1,128)}, u32[]{:S(2)}) copy-start(f32[1,1,512]{2,1,0:T(1,128)} %param.9) | copy-start | bytes 6148
  108.6 1.4 copy-start.2
  112.5 2.4 %copy-start.1 = (bf16[32,16,1024]{2,0,1:T(8,128)(2,1)S(1)}, bf16[32,16,1024]{2,0,1:T(8,128)(2,1)}, u32[]{:S(2)}) copy-start(bf16[32,16,1024]{2,0,1:T(8,128)(2,1)} %copy-done) | copy-start | bytes 3145732
where the time goes:
time: 174 us
  blocking collectives  96.1 us (55%)
  waiting for transfers between devices  22.2 us (13%)
  starting transfers between devices  15.4 us (9%)
  matrix products  13.7 us (8%)
  other arithmetic  13.6 us (8%)
  local copies, waits for them, and re-layouts  11.7 us (7%)
    all_to_all x1, blocking collectives, on_device(): lax.all_to_all(updated, 'mem', split_axis=0, concat_axis=1, tiled=True)  55.2 us
    all_to_all x1, blocking collectives, on_device(): lax.all_to_all(background, 'mem', split_axis=1, concat_axis=0, tiled=True)  40.9 us
    ppermute x3, waiting for transfers between devices, with_halo(): before = lax.ppermute(last, axis, up)  12.5 us
    ppermute x3, starting transfers between devices, with_halo(): before = lax.ppermute(last, axis, up)  11 us
    ppermute x3, waiting for transfers between devices, with_halo(): after = lax.ppermute(initial, axis, down)  9.64 us
    mul x2, other arithmetic, on_device(): states = states * inside[None, None, :, None]  5.26 us
    concatenate x3, other arithmetic, with_halo(): value = jnp.concatenate([before, value, after], axis=dim)  4.55 us
    ppermute x3, starting transfers between devices, with_halo(): after = lax.ppermute(initial, axis, down)  4.35 us
  transfers between devices with their start and end apart: 6, of which 4 were waited for; matrix products, arithmetic and copies ran while one was open for 1% of the time, Pallas kernels for 0%

commit v1 on v0

v1 whole, which is shorter than its diff:
```python
import functools

import jax
import jax.numpy as jnp
from jax import lax
from jax.experimental import pallas as pl
from jax.experimental.pallas import tpu as pltpu
from jax.sharding import PartitionSpec as P

ITERS = 6
SUB = 3
ADVECT = 0.3
VERTICAL = 0.1
PARTS = 16
LOCAL = 32
LEVELS = 4
ROWS = 32
LANES = 128
MEMBERS = 512
NOBS = 512
CHUNKS = 4
WIDE = 256
PITCH = 40
MESH = pl.DeviceIdType.MESH
F32 = jnp.float32
BF16 = jnp.bfloat16


def row_ids():
    return lax.broadcasted_iota(jnp.int32, (8, LANES), 0)


def place(tiles, source, target):
    first, last = source // 8, (source + 2) // 8
    shift = (target - source) % 8
    out = pltpu.roll(tiles[first], shift, 0) if shift else tiles[first]
    if last != first:
        other = pltpu.roll(tiles[last], shift, 0) if shift else tiles[last]
        out = jnp.where(row_ids() >= target + 8 * last - source, other, out)
    return out


def pack(pieces, base):
    rows = row_ids()
    out = []
    for block in range(3):
        acc = jnp.zeros((8, LANES), F32)
        for number, piece in enumerate(pieces):
            low, high = 3 * number - 8 * block, 3 * number + 3 - 8 * block
            if high <= 0 or low >= 8:
                continue
            shift = (3 * number - base) % 8
            moved = pltpu.roll(piece, shift, 0) if shift else piece
            acc = jnp.where((rows >= low) & (rows < high), moved, acc)
        out.append(acc)
    return out


def kernel(
    ens_hbm, dif_ref, cells_ref, values_ref, weights_ref, out_ref,
    ens, up_send, down_send, top_halo, low_halo, coef, turn,
    oc, cell_send, cell_recv, pred_send, pred_recv,
    ymat, zmat, mmat, root, drive, back_send, back_recv,
    load_sem, halo_ssem, halo_rsem, oc_ssem, oc_rsem, pred_ssem, pred_rsem,
    cell_ssem, cell_rsem, back_ssem, back_rsem,
):
    me = lax.axis_index("mem")
    tile = lax.axis_index("tile")
    tiles = lax.axis_size("tile")
    right, left = lax.rem(tile + 1, tiles), lax.rem(tile + tiles - 1, tiles)

    load = pltpu.make_async_copy(ens_hbm, ens, load_sem)
    load.start()
    barrier = pltpu.get_barrier_semaphore()
    for offset in range(1, PARTS):
        pl.semaphore_signal(
            barrier, inc=1, device_id={"mem": lax.rem(me + offset, PARTS)}, device_id_type=MESH
        )
    for other in (left, right):
        pl.semaphore_signal(barrier, inc=1, device_id={"tile": other}, device_id_type=MESH)
    load.wait()

    def pack_pair(pair, carry):
        tops, lows = [], []
        for half in range(2):
            for level in range(LEVELS):
                tops.append(ens[2 * pair + half, level, 0:8, :])
                lows.append(ens[2 * pair + half, level, ROWS - 8 : ROWS, :])
        for block, value in enumerate(pack(tops, 0)):
            up_send[pair, 8 * block : 8 * block + 8, :] = value
        for block, value in enumerate(pack(lows, 5)):
            down_send[pair, 8 * block : 8 * block + 8, :] = value
        return carry

    lax.fori_loop(0, LOCAL // 2, pack_pair, 0)
    tops = [dif_ref[level, 0:8, :] for level in range(LEVELS)]
    lows = [dif_ref[level, ROWS - 8 : ROWS, :] for level in range(LEVELS)]
    for block, value in enumerate(pack(tops, 0)):
        up_send[LOCAL // 2, 8 * block : 8 * block + 8, :] = value
    for block, value in enumerate(pack(lows, 5)):
        down_send[LOCAL // 2, 8 * block : 8 * block + 8, :] = value

    pl.semaphore_wait(barrier, PARTS + 1)

    def remote(source, target, ssem, rsem, device):
        return pltpu.make_async_remote_copy(
            src_ref=source, dst_ref=target, send_sem=ssem, recv_sem=rsem,
            device_id=device, device_id_type=MESH,
        )

    def oc_copy(offset):
        return remote(
            cells_ref.at[0], oc.at[me], oc_ssem.at[offset], oc_rsem.at[offset],
            {"mem": lax.rem(me + offset, PARTS)},
        )

    def pred_copy(offset):
        other = lax.rem(me + offset, PARTS)
        return remote(
            pred_send.at[other], pred_recv.at[me], pred_ssem.at[offset], pred_rsem.at[offset],
            {"mem": other},
        )

    def cell_copy(chunk, offset):
        other = lax.rem(me + offset, PARTS)
        return remote(
            cell_send.at[other, chunk], cell_recv.at[chunk, me],
            cell_ssem.at[chunk, offset], cell_rsem.at[chunk, offset], {"mem": other},
        )

    def back_copy(chunk, offset):
        other = lax.rem(me + offset, PARTS)
        return remote(
            back_send.at[chunk, other], back_recv.at[chunk, me],
            back_ssem.at[chunk, offset], back_rsem.at[chunk, offset], {"mem": other},
        )

    def each(action):
        def step(offset, carry):
            action(offset)
            return carry

        lax.fori_loop(1, PARTS, step, 0)

    to_right = remote(down_send, top_halo, halo_ssem.at[0], halo_rsem.at[0], {"tile": right})
    to_left = remote(up_send, low_halo, halo_ssem.at[1], halo_rsem.at[1], {"tile": left})
    to_right.start()
    to_left.start()
    each(lambda offset: oc_copy(offset).start())
    oc[me] = cells_ref[0]

    top_mask = jnp.where(tile > 0, 1.0, 0.0).astype(F32)
    low_mask = jnp.where(tile < tiles - 1, 1.0, 0.0).astype(F32)
    to_right.wait()
    to_left.wait()
    extra = [
        [halo[LOCAL // 2, 8 * block : 8 * block + 8, :] for block in range(3)]
        for halo in (top_halo, low_halo)
    ]
    lane = lax.broadcasted_iota(jnp.int32, (ROWS + 16, LANES), 1)
    for level in range(LEVELS):
        dif = jnp.concatenate(
            [place(extra[0], 3 * level, 5), dif_ref[level], place(extra[1], 3 * level, 0)], axis=0
        )
        coef[0, level] = 1.0 - ADVECT - 2.0 * VERTICAL - 4.0 * dif
        coef[1, level] = dif + ADVECT
        coef[2, level] = dif
        coef[3, level] = jnp.where(lane == 0, 0.0, dif)
        coef[4, level] = jnp.where(lane == LANES - 1, 0.0, dif)

    def forecast_pair(pair, carry):
        above = [top_halo[pair, 8 * block : 8 * block + 8, :] for block in range(3)]
        below = [low_halo[pair, 8 * block : 8 * block + 8, :] for block in range(3)]
        for half in range(2):
            member = 2 * pair + half
            states = []
            for level in range(LEVELS):
                at = 3 * (LEVELS * half + level)
                states.append(
                    jnp.concatenate(
                        [
                            place(above, at, 5) * top_mask,
                            ens[member, level],
                            place(below, at, 0) * low_mask,
                        ],
                        axis=0,
                    )
                )
            for repeat in range(SUB):
                updated = []
                for level in range(LEVELS):
                    state = states[level]
                    near = [states[n] for n in (level - 1, level + 1) if 0 <= n < LEVELS]
                    column = near[0] + near[1] if len(near) == 2 else near[0]
                    value = (
                        coef[0, level] * state
                        + coef[1, level] * pltpu.roll(state, 1, 0)
                        + coef[2, level] * pltpu.roll(state, ROWS + 15, 0)
                        + coef[3, level] * pltpu.roll(state, 1, 1)
                        + coef[4, level] * pltpu.roll(state, LANES - 1, 1)
                        + VERTICAL * column
                    )
                    if repeat < SUB - 1:
                        value = jnp.concatenate(
                            [
                                value[0:8] * top_mask,
                                value[8 : ROWS + 8],
                                value[ROWS + 8 :] * low_mask,
                            ],
                            axis=0,
                        )
                    updated.append(value)
                states = updated
            for level in range(LEVELS):
                for block in range(ROWS // 8):
                    first = (level * ROWS + 8 * block) * PITCH
                    turn[pl.ds(first + member, 8, stride=PITCH), :] = states[level][
                        8 * block + 8 : 8 * block + 16
                    ]
        return carry

    lax.fori_loop(0, LOCAL // 2, forecast_pair, 0)

    def to_cells(part, carry):
        for chunk in range(CHUNKS):
            for half in range(2):
                first = pl.multiple_of((part * 8 + 2 * chunk + half) * PITCH, 8)
                cell_send[part, chunk, :, half * LANES : (half + 1) * LANES] = turn[
                    pl.ds(first, LOCAL), :
                ].astype(BF16)
        return carry

    lax.fori_loop(0, PARTS, to_cells, 0)

    each(lambda offset: oc_copy(offset).wait())
    within = lax.broadcasted_iota(jnp.int32, (WIDE, NOBS), 0)

    def gather(offset, carry):
        part = lax.rem(me + offset, PARTS)
        index = oc[part]
        hot = jnp.where(within == jnp.bitwise_and(index, WIDE - 1), 1.0, 0.0).astype(BF16)
        group = jnp.broadcast_to(jnp.right_shift(index, 8), (LOCAL, NOBS))
        pieces = []
        for step in (PARTS - 1, 0, 1):
            other = lax.rem(part + step, PARTS)
            for chunk in range(CHUNKS):
                pieces.append(cell_send[other, chunk])
        found = jnp.dot(jnp.concatenate(pieces, axis=0), hot, preferred_element_type=F32)
        total = jnp.zeros((LOCAL, NOBS), F32)
        for number in range(3 * CHUNKS):
            total += jnp.where(
                group == number, found[LOCAL * number : LOCAL * number + LOCAL], 0.0
            )
        pred_send[part] = total.astype(BF16)
        pl.when(offset > 1)(lambda: pred_copy(offset - 1).start())
        return carry

    lax.fori_loop(1, PARTS + 1, gather, 0)
    for chunk in range(CHUNKS):
        each(lambda offset: cell_copy(chunk, offset).start())
        cell_recv[chunk, me] = cell_send[me, chunk]
    pred_recv[me] = pred_send[me]

    each(lambda offset: pred_copy(offset).wait())
    weights, values = weights_ref[0], values_ref[0]
    total = jnp.zeros((1, NOBS), F32)
    for part in range(PARTS):
        total += jnp.sum(pred_recv[part].astype(F32), axis=0, keepdims=True)
    pmean = total * (1.0 / MEMBERS)
    pull = weights * (values - pmean)
    for part in range(PARTS):
        rows = slice(LOCAL * part, LOCAL * part + LOCAL)
        ppert = pred_recv[part].astype(F32) - pmean
        ymat[rows, :] = (ppert * weights).astype(BF16)
        zmat[rows, :] = ppert.astype(BF16)
        drive[rows, :] = jnp.sum(ppert * pull, axis=1, keepdims=True) * (1.0 / (MEMBERS - 1.0))
    gram = lax.dot_general(
        zmat[...], ymat[...], (((1,), (1,)), ((), ())), preferred_element_type=F32
    )
    eye = jnp.where(
        lax.broadcasted_iota(jnp.int32, (MEMBERS, MEMBERS), 0)
        == lax.broadcasted_iota(jnp.int32, (MEMBERS, MEMBERS), 1),
        1.0,
        0.0,
    )
    root[...] = gram * (1.0 / (MEMBERS - 1.0)) + eye
    small = jnp.where(
        lax.broadcasted_iota(jnp.int32, (LANES, LANES), 0)
        == lax.broadcasted_iota(jnp.int32, (LANES, LANES), 1),
        1.0,
        0.0,
    )
    trace = jnp.zeros((1, 1), F32)
    for block in range(MEMBERS // LANES):
        part = slice(LANES * block, LANES * block + LANES)
        diagonal = jnp.sum(root[part, part] * small, axis=1, keepdims=True)
        trace += jnp.sum(diagonal, axis=0, keepdims=True)
    scale = trace * (3.0 / MEMBERS)
    first = (root[...] * (1.0 / scale)).astype(BF16)
    ymat[...] = first
    mmat[...] = (1.5 * eye - 0.5 * first.astype(F32)).astype(BF16)
    zmat[...] = mmat[...]
    ymat[...] = jnp.dot(mmat[...], first, preferred_element_type=F32).astype(BF16)

    def newton(step, carry):
        product = jnp.dot(ymat[...], zmat[...], preferred_element_type=F32)
        mmat[...] = (1.5 * eye - 0.5 * product).astype(BF16)
        ynext = jnp.dot(mmat[...], ymat[...], preferred_element_type=F32).astype(BF16)
        znext = jnp.dot(zmat[...], mmat[...], preferred_element_type=F32).astype(BF16)
        ymat[...] = ynext
        zmat[...] = znext
        return carry

    lax.fori_loop(0, ITERS - 2, newton, 0)
    product = jnp.dot(ymat[...], zmat[...], preferred_element_type=F32)
    mmat[...] = (1.5 * eye - 0.5 * product).astype(BF16)
    root[...] = jnp.dot(zmat[...], mmat[...], preferred_element_type=F32) * (
        1.0 / jnp.sqrt(scale)
    )
    across = jnp.sum(root[...] * drive[...], axis=0, keepdims=True)
    wmean = jnp.zeros((1, MEMBERS), F32)
    for block in range(MEMBERS // LANES):
        part = slice(LANES * block, LANES * block + LANES)
        down = jnp.sum(across[:, part] * small, axis=1, keepdims=True)
        wmean += jnp.sum(root[part, :] * down, axis=0, keepdims=True)
    ymat[...] = (root[...] + wmean).astype(BF16)

    for chunk in range(CHUNKS):
        each(lambda offset: cell_copy(chunk, offset).wait())
        total = jnp.zeros((1, WIDE), F32)
        for part in range(PARTS):
            total += jnp.sum(cell_recv[chunk, part].astype(F32), axis=0, keepdims=True)
        xmean = total * (1.0 / MEMBERS)
        for part in range(PARTS):
            zmat[LOCAL * part : LOCAL * part + LOCAL, 0:WIDE] = (
                cell_recv[chunk, part].astype(F32) - xmean
            ).astype(BF16)
        update = jnp.dot(ymat[...], zmat[:, 0:WIDE], preferred_element_type=F32) + xmean
        for part in range(PARTS):
            back_send[chunk, part] = update[LOCAL * part : LOCAL * part + LOCAL].astype(BF16)
        each(lambda offset: back_copy(chunk, offset).start())
        back_recv[chunk, me] = back_send[chunk, me]

    for chunk in range(CHUNKS):
        each(lambda offset: back_copy(chunk, offset).wait())

        def from_cells(part, carry):
            for half in range(2):
                first = pl.multiple_of((part * 8 + 2 * chunk + half) * PITCH, 8)
                turn[pl.ds(first, LOCAL), :] = back_recv[
                    chunk, part, :, half * LANES : (half + 1) * LANES
                ].astype(F32)
            return carry

        lax.fori_loop(0, PARTS, from_cells, 0)

    def to_states(member, carry):
        for part in range(PARTS):
            out_ref[member, part // 4, (part % 4) * 8 : (part % 4) * 8 + 8, :] = turn[
                pl.ds(part * 8 * PITCH + member, 8, stride=PITCH), :
            ]
        return carry

    lax.fori_loop(0, LOCAL, to_states, 0)


def on_device(ensemble, diffusion, obs_cells, obs_values, obs_weights):
    vmem = pl.BlockSpec(memory_space=pltpu.VMEM)
    dma = pltpu.SemaphoreType.DMA
    halo = pltpu.VMEM((LOCAL // 2 + 1, 24, LANES), F32)
    square = pltpu.VMEM((MEMBERS, MEMBERS), BF16)
    return pl.pallas_call(
        kernel,
        name="cycle",
        out_shape=jax.ShapeDtypeStruct(ensemble.shape, F32),
        in_specs=[pl.BlockSpec(memory_space=pl.ANY)] + [vmem] * 4,
        out_specs=vmem,
        scratch_shapes=[
            pltpu.VMEM(ensemble.shape, F32),
            halo, halo, halo, halo,
            pltpu.VMEM((5, LEVELS, ROWS + 16, LANES), F32),
            pltpu.VMEM((LEVELS * ROWS * PITCH, LANES), F32),
            pltpu.VMEM((PARTS, 1, NOBS), jnp.int32),
            pltpu.VMEM((PARTS, CHUNKS, LOCAL, WIDE), BF16),
            pltpu.VMEM((CHUNKS, PARTS, LOCAL, WIDE), BF16),
            pltpu.VMEM((PARTS, LOCAL, NOBS), BF16),
            pltpu.VMEM((PARTS, LOCAL, NOBS), BF16),
            square, square, square,
            pltpu.VMEM((MEMBERS, MEMBERS), F32),
            pltpu.VMEM((MEMBERS, 1), F32),
            pltpu.VMEM((CHUNKS, PARTS, LOCAL, WIDE), BF16),
            pltpu.VMEM((CHUNKS, PARTS, LOCAL, WIDE), BF16),
            dma, dma((2,)), dma((2,)),
            dma((PARTS,)), dma((PARTS,)), dma((PARTS,)), dma((PARTS,)),
            dma((CHUNKS, PARTS)), dma((CHUNKS, PARTS)),
            dma((CHUNKS, PARTS)), dma((CHUNKS, PARTS)),
        ],
        compiler_params=pltpu.CompilerParams(
            collective_id=0, has_side_effects=True, vmem_limit_bytes=56 * 1024 * 1024
        ),
    )(ensemble, diffusion, obs_cells, obs_values, obs_weights)


def solution(mesh):
    return jax.shard_map(
        on_device,
        mesh=mesh,
        in_specs=(
            P("mem", None, "tile", None),
            P(None, "tile", None),
            P("tile", "mem", None),
            P("tile", "mem", None),
            P("tile", "mem", None),
        ),
        out_specs=P("mem", None, "tile", None),
        check_vma=False,
    )
```

time: 174 us -> 100 us (0.57)
  the two profiles are of different devices: /device:TPU:31 before, /device:TPU:1 now
where the time goes in v1:
time: 100 us
  Pallas kernels  97 us (97%)
  local copies, waits for them, and re-layouts  3.19 us (3%)
    pallas_call x1, Pallas kernels, on_device(): pl.pallas_call(kernel, name='cycle', out_shape=jax.ShapeDtypeStruct(ensem...  97 us
    unnamed x1, local copies, waits for them, and re-layouts  3.19 us

profile of v1, /device:TPU:1, one launch (start us, length us, event | category | flops | bytes accessed | tf_op | source)
XLA Modules:
  0.0 100.2 jit_solution(15075007190593180650)
XLA Ops:
  0.0 97.0 %cycle.1 = f32[32,4,32,128]{3,2,1,0:T(8,128)} custom-call(f32[32,4,32,128]{3,2,1,0:T(8,128)} %ens_hbm.1, f32[4,32,128]{2,1,0:T(8,128)} %dif_ref.1, s32[1,1,512]{2,1,0:T(1,128)} %cells_ref.1, f32[1,1,512]{2,1,0:T(1,128)} %values_ref.1, f32[1,1,512]{2,1,0:T(1,128)} %weights_ref.1), custom_call_target="tpu_custom_call" | custom-call | tf_op jit(solution)/shard_map/cycle/pallas_call | solution.py:372
  97.0 3.2 %copy.7 = f32[32,4,32,128]{3,2,1,0:T(8,128)} copy(f32[32,4,32,128]{3,2,1,0:T(8,128)} %cycle.1) | data formatting | bytes 4194304

commit v2 on v1

--- a/solution.py
+++ b/solution.py
@@ -56,9 +56,45 @@
     return out
 
 
+def windows(above, upper, lower, below, step):
+    rows = row_ids()
+    shift = 2 - step
+    top = jnp.where(rows < shift, pltpu.roll(above, shift, 0), pltpu.roll(upper, shift, 0))
+    shift = 6 - step
+    low = jnp.where(rows < shift, pltpu.roll(lower, shift, 0), pltpu.roll(below, shift, 0))
+    return jnp.concatenate([top, low], axis=0)
+
+
+def coefficients(coef, dif_ref, rows):
+    lane = lax.broadcasted_iota(jnp.int32, (rows, LANES), 1)
+    for level in range(LEVELS):
+        dif = dif_ref[level]
+        coef[0, level] = 1.0 - ADVECT - 2.0 * VERTICAL - 4.0 * dif
+        coef[1, level] = dif + ADVECT
+        coef[2, level] = dif
+        coef[3, level] = jnp.where(lane == 0, 0.0, dif)
+        coef[4, level] = jnp.where(lane == LANES - 1, 0.0, dif)
+
+
+def column(states, level):
+    near = [states[n] for n in (level - 1, level + 1) if 0 <= n < LEVELS]
+    return near[0] + near[1] if len(near) == 2 else near[0]
+
+
+def substep(coef, level, state, west, east, vertical):
+    return (
+        coef[0, level] * state
+        + coef[1, level] * west
+        + coef[2, level] * east
+        + coef[3, level] * pltpu.roll(state, 1, 1)
+        + coef[4, level] * pltpu.roll(state, LANES - 1, 1)
+        + VERTICAL * vertical
+    )
+
+
 def kernel(
     ens_hbm, dif_ref, cells_ref, values_ref, weights_ref, out_ref,
-    ens, up_send, down_send, top_halo, low_halo, coef, turn,
+    ens, up_send, down_send, top_halo, low_halo, coef, edge_coef, edge_dif, turn,
     oc, cell_send, cell_recv, pred_send, pred_recv,
     ymat, zmat, mmat, root, drive, back_send, back_recv,
     load_sem, halo_ssem, halo_rsem, oc_ssem, oc_rsem, pred_ssem, pred_rsem,
@@ -149,6 +185,66 @@
     each(lambda offset: oc_copy(offset).start())
     oc[me] = cells_ref[0]
 
+    coefficients(coef, dif_ref, ROWS)
+
+    def inner_pair(pair, carry):
+        for half in range(2):
+            member = 2 * pair + half
+            states = [ens[member, level] for level in range(LEVELS)]
+            for repeat in range(SUB):
+                states = [
+                    substep(
+                        coef, level, states[level],
+                        pltpu.roll(states[level], 1, 0),
+                        pltpu.roll(states[level], ROWS - 1, 0),
+                        column(states, level),
+                    )
+                    for level in range(LEVELS)
+                ]
+            for level in range(LEVELS):
+                for block in range(ROWS // 8):
+                    first = (level * ROWS + 8 * block) * PITCH
+                    turn[pl.ds(first + member, 8, stride=PITCH), :] = states[level][
+                        8 * block : 8 * block + 8
+                    ]
+        return carry
+
+    def to_cells(part, low, count):
+        for chunk in range(CHUNKS):
+            for half in range(2):
+                first = pl.multiple_of((part * 8 + 2 * chunk + half) * PITCH + low, 8)
+                cell_send[part, chunk, low : low + count, half * LANES : (half + 1) * LANES] = (
+                    turn[pl.ds(first, count), :].astype(BF16)
+                )
+
+    half_count = LOCAL // 2
+    for low in (0, half_count):
+        lax.fori_loop(low // 2, (low + half_count) // 2, inner_pair, 0)
+
+        def inner_cells(number, carry):
+            to_cells(4 * (number // 2) + 1 + lax.rem(number, 2), low, half_count)
+            return carry
+
+        lax.fori_loop(0, PARTS // 2, inner_cells, 0)
+
+        def inner_send(number, carry):
+            turned = lax.rem(number + lax.div(me + 1, 2), PARTS // 2)
+            part = 4 * lax.div(turned, 2) + 1 + lax.rem(turned, 2)
+            offset = lax.rem(part - me + PARTS, PARTS)
+
+            @pl.when(offset > 0)
+            def _():
+                for chunk in range(CHUNKS):
+                    remote(
+                        cell_send.at[part, chunk, pl.ds(low, half_count)],
+                        cell_recv.at[chunk, me, pl.ds(low, half_count)],
+                        cell_ssem.at[chunk, offset], cell_rsem.at[chunk, offset], {"mem": part},
+                    ).start()
+
+            return carry
+
+        lax.fori_loop(0, PARTS // 2, inner_send, 0)
+
     top_mask = jnp.where(tile > 0, 1.0, 0.0).astype(F32)
     low_mask = jnp.where(tile < tiles - 1, 1.0, 0.0).astype(F32)
     to_right.wait()
@@ -157,80 +253,54 @@
         [halo[LOCAL // 2, 8 * block : 8 * block + 8, :] for block in range(3)]
         for halo in (top_halo, low_halo)
     ]
-    lane = lax.broadcasted_iota(jnp.int32, (ROWS + 16, LANES), 1)
     for level in range(LEVELS):
-        dif = jnp.concatenate(
-            [place(extra[0], 3 * level, 5), dif_ref[level], place(extra[1], 3 * level, 0)], axis=0
-        )
-        coef[0, level] = 1.0 - ADVECT - 2.0 * VERTICAL - 4.0 * dif
-        coef[1, level] = dif + ADVECT
-        coef[2, level] = dif
-        coef[3, level] = jnp.where(lane == 0, 0.0, dif)
-        coef[4, level] = jnp.where(lane == LANES - 1, 0.0, dif)
-
-    def forecast_pair(pair, carry):
+        edge_dif[level] = windows(
+            place(extra[0], 3 * level, 5), dif_ref[level, 0:8],
+            dif_ref[level, ROWS - 8 : ROWS], place(extra[1], 3 * level, 0), 0,
+        )
+    coefficients(edge_coef, edge_dif, 16)
+    edge_row = lax.broadcasted_iota(jnp.int32, (16, LANES), 0)
+    edge_mask = jnp.where(edge_row < 2, top_mask, jnp.where(edge_row >= 14, low_mask, 1.0))
+
+    def edge_pair(pair, carry):
         above = [top_halo[pair, 8 * block : 8 * block + 8, :] for block in range(3)]
         below = [low_halo[pair, 8 * block : 8 * block + 8, :] for block in range(3)]
         for half in range(2):
             member = 2 * pair + half
-            states = []
+            states, wests, easts = [], [], []
             for level in range(LEVELS):
                 at = 3 * (LEVELS * half + level)
-                states.append(
-                    jnp.concatenate(
-                        [
-                            place(above, at, 5) * top_mask,
-                            ens[member, level],
-                            place(below, at, 0) * low_mask,
-                        ],
-                        axis=0,
-                    )
+                parts = (
+                    place(above, at, 5) * top_mask, ens[member, level, 0:8],
+                    ens[member, level, ROWS - 8 : ROWS], place(below, at, 0) * low_mask,
                 )
+                states.append(windows(*parts, 0))
+                wests.append(windows(*parts, -1))
+                easts.append(windows(*parts, 1))
             for repeat in range(SUB):
                 updated = []
                 for level in range(LEVELS):
                     state = states[level]
-                    near = [states[n] for n in (level - 1, level + 1) if 0 <= n < LEVELS]
-                    column = near[0] + near[1] if len(near) == 2 else near[0]
-                    value = (
-                        coef[0, level] * state
-                        + coef[1, level] * pltpu.roll(state, 1, 0)
-                        + coef[2, level] * pltpu.roll(state, ROWS + 15, 0)
-                        + coef[3, level] * pltpu.roll(state, 1, 1)
-                        + coef[4, level] * pltpu.roll(state, LANES - 1, 1)
-                        + VERTICAL * column
+                    west = pltpu.roll(state, 1, 0) if repeat else wests[level]
+                    east = pltpu.roll(state, 15, 0) if repeat else easts[level]
+                    value = substep(
+                        edge_coef, level, state, west, east, column(states, level)
                     )
-                    if repeat < SUB - 1:
-                        value = jnp.concatenate(
-                            [
-                                value[0:8] * top_mask,
-                                value[8 : ROWS + 8],
-                                value[ROWS + 8 :] * low_mask,
-                            ],
-                            axis=0,
-                        )
-                    updated.append(value)
+                    updated.append(value * edge_mask if repeat < SUB - 1 else value)
                 states = updated
             for level in range(LEVELS):
-                for block in range(ROWS // 8):
-                    first = (level * ROWS + 8 * block) * PITCH
-                    turn[pl.ds(first + member, 8, stride=PITCH), :] = states[level][
-                        8 * block + 8 : 8 * block + 16
-                    ]
-        return carry
-
-    lax.fori_loop(0, LOCAL // 2, forecast_pair, 0)
-
-    def to_cells(part, carry):
-        for chunk in range(CHUNKS):
-            for half in range(2):
-                first = pl.multiple_of((part * 8 + 2 * chunk + half) * PITCH, 8)
-                cell_send[part, chunk, :, half * LANES : (half + 1) * LANES] = turn[
-                    pl.ds(first, LOCAL), :
-                ].astype(BF16)
-        return carry
-
-    lax.fori_loop(0, PARTS, to_cells, 0)
+                first = level * ROWS * PITCH + member
+                turn[pl.ds(first, 3, stride=PITCH), :] = states[level][2:5]
+                turn[pl.ds(first + (ROWS - 3) * PITCH, 3, stride=PITCH), :] = states[level][11:14]
+        return carry
+
+    lax.fori_loop(0, LOCAL // 2, edge_pair, 0)
+
+    def edge_cells(number, carry):
+        to_cells(4 * (number // 2) + 3 * lax.rem(number, 2), 0, LOCAL)
+        return carry
+
+    lax.fori_loop(0, PARTS // 2, edge_cells, 0)
 
     each(lambda offset: oc_copy(offset).wait())
     within = lax.broadcasted_iota(jnp.int32, (WIDE, NOBS), 0)
@@ -257,7 +327,14 @@
 
     lax.fori_loop(1, PARTS + 1, gather, 0)
     for chunk in range(CHUNKS):
-        each(lambda offset: cell_copy(chunk, offset).start())
+        def edge_send(number, carry):
+            turned = lax.rem(number + lax.div(me + 1, 2), PARTS // 2)
+            part = 4 * lax.div(turned, 2) + 3 * lax.rem(turned, 2)
+            offset = lax.rem(part - me + PARTS, PARTS)
+            pl.when(offset > 0)(lambda: cell_copy(chunk, offset).start())
+            return carry
+
+        lax.fori_loop(0, PARTS // 2, edge_send, 0)
         cell_recv[chunk, me] = cell_send[me, chunk]
     pred_recv[me] = pred_send[me]
 
@@ -372,13 +449,15 @@
     return pl.pallas_call(
         kernel,
         name="cycle",
-        out_shape=jax.ShapeDtypeStruct(ensemble.shape, F32),
+        out_shape=pltpu.VMEM(ensemble.shape, F32),
         in_specs=[pl.BlockSpec(memory_space=pl.ANY)] + [vmem] * 4,
         out_specs=vmem,
         scratch_shapes=[
             pltpu.VMEM(ensemble.shape, F32),
             halo, halo, halo, halo,
-            pltpu.VMEM((5, LEVELS, ROWS + 16, LANES), F32),
+            pltpu.VMEM((5, LEVELS, ROWS, LANES), F32),
+            pltpu.VMEM((5, LEVELS, 16, LANES), F32),
+            pltpu.VMEM((LEVELS, 16, LANES), F32),
             pltpu.VMEM((LEVELS * ROWS * PITCH, LANES), F32),
             pltpu.VMEM((PARTS, 1, NOBS), jnp.int32),
             pltpu.VMEM((PARTS, CHUNKS, LOCAL, WIDE), BF16),

time: 100 us -> 82.4 us (0.82)
  Pallas kernels: 97 us -> 80.9 us
  local copies, waits for them, and re-layouts: 3.19 us -> 1.32 us
    pallas_call x1, Pallas kernels: 97 us -> 80.9 us  [on_device(): pl.pallas_call(kernel, name='cycle', out_shape=pltpu.VMEM(ensemble.shape,...]
    unnamed x1, local copies, waits for them, and re-layouts: 3.19 us -> 1.32 us
where the time goes in v2:
time: 82.4 us; the launch traced here: 82.2 us
  Pallas kernels  80.9 us (98%)
  local copies, waits for them, and re-layouts  1.32 us (2%)
    pallas_call x1, Pallas kernels, on_device(): pl.pallas_call(kernel, name='cycle', out_shape=pltpu.VMEM(ensemble.shape,...  80.9 us

profile of v2, /device:TPU:1, one launch (start us, length us, event | category | flops | bytes accessed | tf_op | source)
XLA Modules:
  0.0 82.2 jit_solution(14866799544451757703)
XLA Ops:
  0.0 80.9 %cycle.1 = f32[32,4,32,128]{3,2,1,0:T(8,128)S(1)} custom-call(f32[32,4,32,128]{3,2,1,0:T(8,128)} %ens_hbm.1, f32[4,32,128]{2,1,0:T(8,128)} %dif_ref.1, s32[1,1,512]{2,1,0:T(1,128)} %cells_ref.1, f32[1,1,512]{2,1,0:T(1,128)} %values_ref.1, f32[1,1,512]{2,1,0:T(1,128)} %weights_ref.1), custom_call_target="tpu_custom_call" | custom-call | tf_op jit(solution)/shard_map/cycle/pallas_call | solution.py:449
  80.9 1.3 %copy.7 = f32[32,4,32,128]{3,2,1,0:T(8,128)} copy(f32[32,4,32,128]{3,2,1,0:T(8,128)S(1)} %cycle.1) | data formatting | bytes 4194304

commit v3 on v2

--- a/solution.py
+++ b/solution.py
@@ -93,9 +93,9 @@
 
 
 def kernel(
-    ens_hbm, dif_ref, cells_ref, values_ref, weights_ref, out_ref,
-    ens, up_send, down_send, top_halo, low_halo, coef, edge_coef, edge_dif, turn,
-    oc, cell_send, cell_recv, pred_send, pred_recv,
+    ens_hbm, dif_hbm, cells_hbm, values_hbm, weights_hbm, out_ref,
+    ens, dif_ref, cells_ref, values_ref, weights_ref, up_send, down_send, top_halo, low_halo, coef, edge_coef, edge_dif, turn,
+    oc, hot, cell_send, cell_recv, pred_send, pred_recv,
     ymat, zmat, mmat, root, drive, back_send, back_recv,
     load_sem, halo_ssem, halo_rsem, oc_ssem, oc_rsem, pred_ssem, pred_rsem,
     cell_ssem, cell_rsem, back_ssem, back_rsem,
@@ -105,8 +105,22 @@
     tiles = lax.axis_size("tile")
     right, left = lax.rem(tile + 1, tiles), lax.rem(tile + tiles - 1, tiles)
 
-    load = pltpu.make_async_copy(ens_hbm, ens, load_sem)
-    load.start()
+    half_count = LOCAL // 2
+    loads = [
+        pltpu.make_async_copy(source, target, load_sem.at[number])
+        for number, (source, target) in enumerate(
+            [
+                (dif_hbm, dif_ref),
+                (ens_hbm.at[0:half_count], ens.at[0:half_count]),
+                (ens_hbm.at[half_count:LOCAL], ens.at[half_count:LOCAL]),
+                (cells_hbm, cells_ref),
+                (values_hbm, values_ref),
+                (weights_hbm, weights_ref),
+            ]
+        )
+    ]
+    for load in loads:
+        load.start()
     barrier = pltpu.get_barrier_semaphore()
     for offset in range(1, PARTS):
         pl.semaphore_signal(
@@ -114,77 +128,7 @@
         )
     for other in (left, right):
         pl.semaphore_signal(barrier, inc=1, device_id={"tile": other}, device_id_type=MESH)
-    load.wait()
-
-    def pack_pair(pair, carry):
-        tops, lows = [], []
-        for half in range(2):
-            for level in range(LEVELS):
-                tops.append(ens[2 * pair + half, level, 0:8, :])
-                lows.append(ens[2 * pair + half, level, ROWS - 8 : ROWS, :])
-        for block, value in enumerate(pack(tops, 0)):
-            up_send[pair, 8 * block : 8 * block + 8, :] = value
-        for block, value in enumerate(pack(lows, 5)):
-            down_send[pair, 8 * block : 8 * block + 8, :] = value
-        return carry
-
-    lax.fori_loop(0, LOCAL // 2, pack_pair, 0)
-    tops = [dif_ref[level, 0:8, :] for level in range(LEVELS)]
-    lows = [dif_ref[level, ROWS - 8 : ROWS, :] for level in range(LEVELS)]
-    for block, value in enumerate(pack(tops, 0)):
-        up_send[LOCAL // 2, 8 * block : 8 * block + 8, :] = value
-    for block, value in enumerate(pack(lows, 5)):
-        down_send[LOCAL // 2, 8 * block : 8 * block + 8, :] = value
-
-    pl.semaphore_wait(barrier, PARTS + 1)
-
-    def remote(source, target, ssem, rsem, device):
-        return pltpu.make_async_remote_copy(
-            src_ref=source, dst_ref=target, send_sem=ssem, recv_sem=rsem,
-            device_id=device, device_id_type=MESH,
-        )
-
-    def oc_copy(offset):
-        return remote(
-            cells_ref.at[0], oc.at[me], oc_ssem.at[offset], oc_rsem.at[offset],
-            {"mem": lax.rem(me + offset, PARTS)},
-        )
-
-    def pred_copy(offset):
-        other = lax.rem(me + offset, PARTS)
-        return remote(
-            pred_send.at[other], pred_recv.at[me], pred_ssem.at[offset], pred_rsem.at[offset],
-            {"mem": other},
-        )
-
-    def cell_copy(chunk, offset):
-        other = lax.rem(me + offset, PARTS)
-        return remote(
-            cell_send.at[other, chunk], cell_recv.at[chunk, me],
-            cell_ssem.at[chunk, offset], cell_rsem.at[chunk, offset], {"mem": other},
-        )
-
-    def back_copy(chunk, offset):
-        other = lax.rem(me + offset, PARTS)
-        return remote(
-            back_send.at[chunk, other], back_recv.at[chunk, me],
-            back_ssem.at[chunk, offset], back_rsem.at[chunk, offset], {"mem": other},
-        )
-
-    def each(action):
-        def step(offset, carry):
-            action(offset)
-            return carry
-
-        lax.fori_loop(1, PARTS, step, 0)
-
-    to_right = remote(down_send, top_halo, halo_ssem.at[0], halo_rsem.at[0], {"tile": right})
-    to_left = remote(up_send, low_halo, halo_ssem.at[1], halo_rsem.at[1], {"tile": left})
-    to_right.start()
-    to_left.start()
-    each(lambda offset: oc_copy(offset).start())
-    oc[me] = cells_ref[0]
-
+    loads[0].wait()
     coefficients(coef, dif_ref, ROWS)
 
     def inner_pair(pair, carry):
@@ -217,33 +161,117 @@
                     turn[pl.ds(first, count), :].astype(BF16)
                 )
 
-    half_count = LOCAL // 2
-    for low in (0, half_count):
-        lax.fori_loop(low // 2, (low + half_count) // 2, inner_pair, 0)
-
-        def inner_cells(number, carry):
-            to_cells(4 * (number // 2) + 1 + lax.rem(number, 2), low, half_count)
+    def inner_cells(low, number, carry):
+        to_cells(4 * (number // 2) + 1 + lax.rem(number, 2), low, half_count)
+        return carry
+
+    loads[1].wait()
+    lax.fori_loop(0, half_count // 2, inner_pair, 0)
+    lax.fori_loop(0, PARTS // 2, functools.partial(inner_cells, 0), 0)
+    loads[2].wait()
+
+    def pack_pair(pair, carry):
+        tops, lows = [], []
+        for half in range(2):
+            for level in range(LEVELS):
+                tops.append(ens[2 * pair + half, level, 0:8, :])
+                lows.append(ens[2 * pair + half, level, ROWS - 8 : ROWS, :])
+        for block, value in enumerate(pack(tops, 0)):
+            up_send[pair, 8 * block : 8 * block + 8, :] = value
+        for block, value in enumerate(pack(lows, 5)):
+            down_send[pair, 8 * block : 8 * block + 8, :] = value
+        return carry
+
+    lax.fori_loop(0, LOCAL // 2, pack_pair, 0)
+    tops = [dif_ref[level, 0:8, :] for level in range(LEVELS)]
+    lows = [dif_ref[level, ROWS - 8 : ROWS, :] for level in range(LEVELS)]
+    for block, value in enumerate(pack(tops, 0)):
+        up_send[LOCAL // 2, 8 * block : 8 * block + 8, :] = value
+    for block, value in enumerate(pack(lows, 5)):
+        down_send[LOCAL // 2, 8 * block : 8 * block + 8, :] = value
+
+    pl.semaphore_wait(barrier, PARTS + 1)
+
+    def remote(source, target, ssem, rsem, device):
+        return pltpu.make_async_remote_copy(
+            src_ref=source, dst_ref=target, send_sem=ssem, recv_sem=rsem,
+            device_id=device, device_id_type=MESH,
+        )
+
+    def oc_copy(offset):
+        return remote(
+            cells_ref.at[0], oc.at[me], oc_ssem.at[offset], oc_rsem.at[offset],
+            {"mem": lax.rem(me + offset, PARTS)},
+        )
+
+    def pred_copy(offset):
+        other = lax.rem(me + offset, PARTS)
+        return remote(
+            pred_send.at[other], pred_recv.at[me], pred_ssem.at[offset], pred_rsem.at[offset],
+            {"mem": other},
+        )
+
+    def cell_copy(chunk, offset):
+        other = lax.rem(me + offset, PARTS)
+        return remote(
+            cell_send.at[other, chunk], cell_recv.at[chunk, me],
+            cell_ssem.at[chunk, offset], cell_rsem.at[chunk, offset], {"mem": other},
+        )
+
+    def back_copy(chunk, offset):
+        other = lax.rem(me + offset, PARTS)
+        return remote(
+            back_send.at[chunk, other], back_recv.at[chunk, me],
+            back_ssem.at[chunk, offset], back_rsem.at[chunk, offset], {"mem": other},
+        )
+
+    def each(action):
+        def step(offset, carry):
+            action(offset)
             return carry
 
-        lax.fori_loop(0, PARTS // 2, inner_cells, 0)
-
-        def inner_send(number, carry):
-            turned = lax.rem(number + lax.div(me + 1, 2), PARTS // 2)
-            part = 4 * lax.div(turned, 2) + 1 + lax.rem(turned, 2)
-            offset = lax.rem(part - me + PARTS, PARTS)
-
-            @pl.when(offset > 0)
-            def _():
-                for chunk in range(CHUNKS):
-                    remote(
-                        cell_send.at[part, chunk, pl.ds(low, half_count)],
-                        cell_recv.at[chunk, me, pl.ds(low, half_count)],
-                        cell_ssem.at[chunk, offset], cell_rsem.at[chunk, offset], {"mem": part},
-                    ).start()
-
-            return carry
-
-        lax.fori_loop(0, PARTS // 2, inner_send, 0)
+        lax.fori_loop(1, PARTS, step, 0)
+
+    to_right = remote(down_send, top_halo, halo_ssem.at[0], halo_rsem.at[0], {"tile": right})
+    to_left = remote(up_send, low_halo, halo_ssem.at[1], halo_rsem.at[1], {"tile": left})
+    to_right.start()
+    to_left.start()
+    for load in loads[3:]:
+        load.wait()
+    each(lambda offset: oc_copy(offset).start())
+    oc[me] = cells_ref[0]
+
+
+    def inner_send(low, number, carry):
+        turned = lax.rem(number + lax.div(me + 1, 2), PARTS // 2)
+        part = 4 * lax.div(turned, 2) + 1 + lax.rem(turned, 2)
+        offset = lax.rem(part - me + PARTS, PARTS)
+
+        @pl.when(offset > 0)
+        def _():
+            for chunk in range(CHUNKS):
+                remote(
+                    cell_send.at[part, chunk, pl.ds(low, half_count)],
+                    cell_recv.at[chunk, me, pl.ds(low, half_count)],
+                    cell_ssem.at[chunk, offset], cell_rsem.at[chunk, offset], {"mem": part},
+                ).start()
+
+        return carry
+
+    lax.fori_loop(0, PARTS // 2, functools.partial(inner_send, 0), 0)
+    lax.fori_loop(half_count // 2, LOCAL // 2, inner_pair, 0)
+    lax.fori_loop(0, PARTS // 2, functools.partial(inner_cells, half_count), 0)
+    lax.fori_loop(0, PARTS // 2, functools.partial(inner_send, half_count), 0)
+
+    each(lambda offset: oc_copy(offset).wait())
+    within = lax.broadcasted_iota(jnp.int32, (WIDE, NOBS), 0)
+
+    def mark(part, carry):
+        index = jnp.bitwise_and(oc[part], WIDE - 1)
+        hot[part] = jnp.where(within == index, 1.0, 0.0).astype(BF16)
+        return carry
+
+    lax.fori_loop(0, PARTS, mark, 0)
 
     top_mask = jnp.where(tile > 0, 1.0, 0.0).astype(F32)
     low_mask = jnp.where(tile < tiles - 1, 1.0, 0.0).astype(F32)
@@ -262,39 +290,66 @@
     edge_row = lax.broadcasted_iota(jnp.int32, (16, LANES), 0)
     edge_mask = jnp.where(edge_row < 2, top_mask, jnp.where(edge_row >= 14, low_mask, 1.0))
 
-    def edge_pair(pair, carry):
-        above = [top_halo[pair, 8 * block : 8 * block + 8, :] for block in range(3)]
-        below = [low_halo[pair, 8 * block : 8 * block + 8, :] for block in range(3)]
-        for half in range(2):
-            member = 2 * pair + half
-            states, wests, easts = [], [], []
+    edge_top = edge_row == 0
+    edge_low = edge_row == 15
+    rows = row_ids()
+
+    def moved(tiles, source, target, count):
+        first, last = source // 8, (source + count - 1) // 8
+        shift = (target - source) % 8
+        pieces = [
+            pltpu.roll(tiles[n], shift, 0) if shift else tiles[n] for n in (first, last)[: 1 + (last > first)]
+        ]
+        if len(pieces) == 1:
+            return pieces[0]
+        return jnp.where(rows >= target + 8 * last - source, pieces[1], pieces[0])
+
+    def edge_group(group, carry):
+        members = range(4)
+        states, wests, easts = {}, {}, {}
+        for number in members:
+            pair, half = 2 * group + number // 2, number % 2
+            above = [top_halo[pair, 8 * n : 8 * n + 8, :] for n in range(3)]
+            below = [low_halo[pair, 8 * n : 8 * n + 8, :] for n in range(3)]
             for level in range(LEVELS):
                 at = 3 * (LEVELS * half + level)
-                parts = (
-                    place(above, at, 5) * top_mask, ens[member, level, 0:8],
-                    ens[member, level, ROWS - 8 : ROWS], place(below, at, 0) * low_mask,
+                block = (2 * pair + half, level)
+                upper, lower = ens[(*block, slice(0, 8))], ens[(*block, slice(ROWS - 8, ROWS))]
+                top = jnp.where(
+                    rows < 2, moved(above, at + 1, 0, 2) * top_mask, pltpu.roll(upper, 2, 0)
                 )
-                states.append(windows(*parts, 0))
-                wests.append(windows(*parts, -1))
-                easts.append(windows(*parts, 1))
-            for repeat in range(SUB):
-                updated = []
+                low = jnp.where(
+                    rows < 6, pltpu.roll(lower, 6, 0), moved(below, at, 6, 2) * low_mask
+                )
+                state = jnp.concatenate([top, low], axis=0)
+                first = moved(above, at, 0, 1) * top_mask
+                last = moved(below, at + 2, 7, 1) * low_mask
+                states[number, level] = state
+                wests[number, level] = jnp.where(
+                    edge_top, jnp.concatenate([first, low], axis=0), pltpu.roll(state, 1, 0)
+                )
+                easts[number, level] = jnp.where(
+                    edge_low, jnp.concatenate([top, last], axis=0), pltpu.roll(state, 15, 0)
+                )
+        for repeat in range(SUB):
+            updated = {}
+            for number in members:
+                own = [states[number, level] for level in range(LEVELS)]
                 for level in range(LEVELS):
-                    state = states[level]
-                    west = pltpu.roll(state, 1, 0) if repeat else wests[level]
-                    east = pltpu.roll(state, 15, 0) if repeat else easts[level]
-                    value = substep(
-                        edge_coef, level, state, west, east, column(states, level)
-                    )
-                    updated.append(value * edge_mask if repeat < SUB - 1 else value)
-                states = updated
+                    west = pltpu.roll(own[level], 1, 0) if repeat else wests[number, level]
+                    east = pltpu.roll(own[level], 15, 0) if repeat else easts[number, level]
+                    value = substep(edge_coef, level, own[level], west, east, column(own, level))
+                    updated[number, level] = value * edge_mask if repeat < SUB - 1 else value
+            states = updated
+        for number in members:
             for level in range(LEVELS):
-                first = level * ROWS * PITCH + member
-                turn[pl.ds(first, 3, stride=PITCH), :] = states[level][2:5]
-                turn[pl.ds(first + (ROWS - 3) * PITCH, 3, stride=PITCH), :] = states[level][11:14]
-        return carry
-
-    lax.fori_loop(0, LOCAL // 2, edge_pair, 0)
+                first = level * ROWS * PITCH + 4 * group + number
+                value = states[number, level]
+                turn[pl.ds(first, 3, stride=PITCH), :] = value[2:5]
+                turn[pl.ds(first + (ROWS - 3) * PITCH, 3, stride=PITCH), :] = value[11:14]
+        return carry
+
+    lax.fori_loop(0, LOCAL // 4, edge_group, 0)
 
     def edge_cells(number, carry):
         to_cells(4 * (number // 2) + 3 * lax.rem(number, 2), 0, LOCAL)
@@ -302,30 +357,29 @@
 
     lax.fori_loop(0, PARTS // 2, edge_cells, 0)
 
-    each(lambda offset: oc_copy(offset).wait())
-    within = lax.broadcasted_iota(jnp.int32, (WIDE, NOBS), 0)
-
-    def gather(offset, carry):
-        part = lax.rem(me + offset, PARTS)
-        index = oc[part]
-        hot = jnp.where(within == jnp.bitwise_and(index, WIDE - 1), 1.0, 0.0).astype(BF16)
-        group = jnp.broadcast_to(jnp.right_shift(index, 8), (LOCAL, NOBS))
+    def order(number):
+        half = lax.div(number + 1, 2)
+        return jnp.where(lax.rem(number, 2) == 0, PARTS // 2 + half, PARTS // 2 - half)
+
+    def gather(number, carry):
+        part = lax.rem(me + order(number), PARTS)
+        group = jnp.broadcast_to(jnp.right_shift(oc[part], 8), (LOCAL, NOBS))
         pieces = []
         for step in (PARTS - 1, 0, 1):
             other = lax.rem(part + step, PARTS)
             for chunk in range(CHUNKS):
                 pieces.append(cell_send[other, chunk])
-        found = jnp.dot(jnp.concatenate(pieces, axis=0), hot, preferred_element_type=F32)
+        found = jnp.dot(jnp.concatenate(pieces, axis=0), hot[part], preferred_element_type=F32)
         total = jnp.zeros((LOCAL, NOBS), F32)
-        for number in range(3 * CHUNKS):
+        for piece in range(3 * CHUNKS):
             total += jnp.where(
-                group == number, found[LOCAL * number : LOCAL * number + LOCAL], 0.0
+                group == piece, found[LOCAL * piece : LOCAL * piece + LOCAL], 0.0
             )
         pred_send[part] = total.astype(BF16)
-        pl.when(offset > 1)(lambda: pred_copy(offset - 1).start())
-        return carry
-
-    lax.fori_loop(1, PARTS + 1, gather, 0)
+        pl.when(number > 0)(lambda: pred_copy(order(number - 1)).start())
+        return carry
+
+    lax.fori_loop(0, PARTS, gather, 0)
     for chunk in range(CHUNKS):
         def edge_send(number, carry):
             turned = lax.rem(number + lax.div(me + 1, 2), PARTS // 2)
@@ -450,16 +504,21 @@
         kernel,
         name="cycle",
         out_shape=pltpu.VMEM(ensemble.shape, F32),
-        in_specs=[pl.BlockSpec(memory_space=pl.ANY)] + [vmem] * 4,
+        in_specs=[pl.BlockSpec(memory_space=pl.ANY)] * 5,
         out_specs=vmem,
         scratch_shapes=[
             pltpu.VMEM(ensemble.shape, F32),
+            pltpu.VMEM(diffusion.shape, F32),
+            pltpu.VMEM(obs_cells.shape, jnp.int32),
+            pltpu.VMEM(obs_values.shape, F32),
+            pltpu.VMEM(obs_weights.shape, F32),
             halo, halo, halo, halo,
             pltpu.VMEM((5, LEVELS, ROWS, LANES), F32),
             pltpu.VMEM((5, LEVELS, 16, LANES), F32),
             pltpu.VMEM((LEVELS, 16, LANES), F32),
             pltpu.VMEM((LEVELS * ROWS * PITCH, LANES), F32),
             pltpu.VMEM((PARTS, 1, NOBS), jnp.int32),
+            pltpu.VMEM((PARTS, WIDE, NOBS), BF16),
             pltpu.VMEM((PARTS, CHUNKS, LOCAL, WIDE), BF16),
             pltpu.VMEM((CHUNKS, PARTS, LOCAL, WIDE), BF16),
             pltpu.VMEM((PARTS, LOCAL, NOBS), BF16),
@@ -469,7 +528,7 @@
             pltpu.VMEM((MEMBERS, 1), F32),
             pltpu.VMEM((CHUNKS, PARTS, LOCAL, WIDE), BF16),
             pltpu.VMEM((CHUNKS, PARTS, LOCAL, WIDE), BF16),
-            dma, dma((2,)), dma((2,)),
+            dma((6,)), dma((2,)), dma((2,)),
             dma((PARTS,)), dma((PARTS,)), dma((PARTS,)), dma((PARTS,)),
             dma((CHUNKS, PARTS)), dma((CHUNKS, PARTS)),
             dma((CHUNKS, PARTS)), dma((CHUNKS, PARTS)),

time: 82.4 us -> 79.2 us (0.961)
  Pallas kernels: 80.9 us -> 77.7 us
    pallas_call x1, Pallas kernels: 80.9 us -> 77.7 us  [on_device(): pl.pallas_call(kernel, name='cycle', out_shape=pltpu.VMEM(ensemble.shape,...]
where the time goes in v3:
time: 79.2 us; the launch traced here: 79 us
  Pallas kernels  77.7 us (98%)
  local copies, waits for them, and re-layouts  1.32 us (2%)
    pallas_call x1, Pallas kernels, on_device(): pl.pallas_call(kernel, name='cycle', out_shape=pltpu.VMEM(ensemble.shape,...  77.7 us

profile of v3, /device:TPU:1, one launch (start us, length us, event | category | flops | bytes accessed | tf_op | source)
XLA Modules:
  0.0 79.0 jit_solution(2614374791763936461)
XLA Ops:
  0.0 77.7 %cycle.1 = f32[32,4,32,128]{3,2,1,0:T(8,128)S(1)} custom-call(f32[32,4,32,128]{3,2,1,0:T(8,128)} %ens_hbm.1, f32[4,32,128]{2,1,0:T(8,128)} %dif_hbm.1, s32[1,1,512]{2,1,0:T(1,128)} %cells_hbm.1, f32[1,1,512]{2,1,0:T(1,128)} %values_hbm.1, f32[1,1,512]{2,1,0:T(1,128)} %weights_hbm.1), custom_call_target="tpu_custom_call" | custom-call | tf_op jit(solution)/shard_map/cycle/pallas_call | solution.py:503
  77.7 1.3 %copy.7 = f32[32,4,32,128]{3,2,1,0:T(8,128)} copy(f32[32,4,32,128]{3,2,1,0:T(8,128)S(1)} %cycle.1) | data formatting | bytes 4194304

commit v4 on v3

--- a/solution.py
+++ b/solution.py
@@ -97,7 +97,7 @@
     ens, dif_ref, cells_ref, values_ref, weights_ref, up_send, down_send, top_halo, low_halo, coef, edge_coef, edge_dif, turn,
     oc, hot, cell_send, cell_recv, pred_send, pred_recv,
     ymat, zmat, mmat, root, drive, back_send, back_recv,
-    load_sem, halo_ssem, halo_rsem, oc_ssem, oc_rsem, pred_ssem, pred_rsem,
+    ready, load_sem, halo_ssem, halo_rsem, oc_ssem, oc_rsem, pred_ssem, pred_rsem,
     cell_ssem, cell_rsem, back_ssem, back_rsem,
 ):
     me = lax.axis_index("mem")
@@ -122,13 +122,107 @@
     for load in loads:
         load.start()
     barrier = pltpu.get_barrier_semaphore()
-    for offset in range(1, PARTS):
-        pl.semaphore_signal(
-            barrier, inc=1, device_id={"mem": lax.rem(me + offset, PARTS)}, device_id_type=MESH
-        )
+    plane = lax.div(me, 2)
+
+    def greet(offset, carry):
+        other = lax.rem(me + offset, PARTS)
+
+        @pl.when(lax.div(other, 2) >= plane)
+        def _():
+            pl.semaphore_signal(barrier, inc=1, device_id={"mem": other}, device_id_type=MESH)
+
+        return carry
+
+    lax.fori_loop(1, PARTS, greet, 0)
     for other in (left, right):
         pl.semaphore_signal(barrier, inc=1, device_id={"tile": other}, device_id_type=MESH)
-    loads[0].wait()
+    pl.semaphore_wait(barrier, 2 * plane + 3)
+
+    def announce(other, carry):
+        pl.semaphore_signal(
+            ready.at[plane], inc=1, device_id={"mem": other}, device_id_type=MESH
+        )
+        return carry
+
+    lax.fori_loop(0, 2 * plane, announce, 0)
+
+    def remote(source, target, ssem, rsem, device):
+        return pltpu.make_async_remote_copy(
+            src_ref=source, dst_ref=target, send_sem=ssem, recv_sem=rsem,
+            device_id=device, device_id_type=MESH,
+        )
+
+    def oc_copy(offset):
+        return remote(
+            cells_ref.at[0], oc.at[me], oc_ssem.at[offset], oc_rsem.at[offset],
+            {"mem": lax.rem(me + offset, PARTS)},
+        )
+
+    def pred_copy(offset):
+        other = lax.rem(me + offset, PARTS)
+        return remote(
+            pred_send.at[other], pred_recv.at[me], pred_ssem.at[offset], pred_rsem.at[offset],
+            {"mem": other},
+        )
+
+    def cell_copy(chunk, offset):
+        other = lax.rem(me + offset, PARTS)
+        return remote(
+            cell_send.at[other, chunk], cell_recv.at[chunk, me],
+            cell_ssem.at[chunk, offset], cell_rsem.at[chunk, offset], {"mem": other},
+        )
+
+    def back_copy(chunk, offset):
+        other = lax.rem(me + offset, PARTS)
+        return remote(
+            back_send.at[chunk, other], back_recv.at[chunk, me],
+            back_ssem.at[chunk, offset], back_rsem.at[chunk, offset], {"mem": other},
+        )
+
+    def each(action):
+        def step(offset, carry):
+            action(offset)
+            return carry
+
+        lax.fori_loop(1, PARTS, step, 0)
+
+    to_right = remote(down_send, top_halo, halo_ssem.at[0], halo_rsem.at[0], {"tile": right})
+    to_left = remote(up_send, low_halo, halo_ssem.at[1], halo_rsem.at[1], {"tile": left})
+    for load in loads[3:]:
+        load.wait()
+    oc[me] = cells_ref[0]
+
+    def oc_early(offset):
+        pl.when(lax.div(lax.rem(me + offset, PARTS), 2) <= plane)(
+            lambda: oc_copy(offset).start()
+        )
+
+    each(oc_early)
+    for load in loads[:3]:
+        load.wait()
+
+    def pack_pair(pair, carry):
+        tops, lows = [], []
+        for half in range(2):
+            for level in range(LEVELS):
+                tops.append(ens[2 * pair + half, level, 0:8, :])
+                lows.append(ens[2 * pair + half, level, ROWS - 8 : ROWS, :])
+        for block, value in enumerate(pack(tops, 0)):
+            up_send[pair, 8 * block : 8 * block + 8, :] = value
+        for block, value in enumerate(pack(lows, 5)):
+            down_send[pair, 8 * block : 8 * block + 8, :] = value
+        return carry
+
+    lax.fori_loop(0, LOCAL // 2, pack_pair, 0)
+    tops = [dif_ref[level, 0:8, :] for level in range(LEVELS)]
+    lows = [dif_ref[level, ROWS - 8 : ROWS, :] for level in range(LEVELS)]
+    for block, value in enumerate(pack(tops, 0)):
+        up_send[LOCAL // 2, 8 * block : 8 * block + 8, :] = value
+    for block, value in enumerate(pack(lows, 5)):
+        down_send[LOCAL // 2, 8 * block : 8 * block + 8, :] = value
+    to_right.start()
+    to_left.start()
+
     coefficients(coef, dif_ref, ROWS)
 
     def inner_pair(pair, carry):
@@ -165,89 +259,15 @@
         to_cells(4 * (number // 2) + 1 + lax.rem(number, 2), low, half_count)
         return carry
 
-    loads[1].wait()
     lax.fori_loop(0, half_count // 2, inner_pair, 0)
     lax.fori_loop(0, PARTS // 2, functools.partial(inner_cells, 0), 0)
-    loads[2].wait()
-
-    def pack_pair(pair, carry):
-        tops, lows = [], []
-        for half in range(2):
-            for level in range(LEVELS):
-                tops.append(ens[2 * pair + half, level, 0:8, :])
-                lows.append(ens[2 * pair + half, level, ROWS - 8 : ROWS, :])
-        for block, value in enumerate(pack(tops, 0)):
-            up_send[pair, 8 * block : 8 * block + 8, :] = value
-        for block, value in enumerate(pack(lows, 5)):
-            down_send[pair, 8 * block : 8 * block + 8, :] = value
-        return carry
-
-    lax.fori_loop(0, LOCAL // 2, pack_pair, 0)
-    tops = [dif_ref[level, 0:8, :] for level in range(LEVELS)]
-    lows = [dif_ref[level, ROWS - 8 : ROWS, :] for level in range(LEVELS)]
-    for block, value in enumerate(pack(tops, 0)):
-        up_send[LOCAL // 2, 8 * block : 8 * block + 8, :] = value
-    for block, value in enumerate(pack(lows, 5)):
-        down_send[LOCAL // 2, 8 * block : 8 * block + 8, :] = value
-
-    pl.semaphore_wait(barrier, PARTS + 1)
-
-    def remote(source, target, ssem, rsem, device):
-        return pltpu.make_async_remote_copy(
-            src_ref=source, dst_ref=target, send_sem=ssem, recv_sem=rsem,
-            device_id=device, device_id_type=MESH,
-        )
-
-    def oc_copy(offset):
-        return remote(
-            cells_ref.at[0], oc.at[me], oc_ssem.at[offset], oc_rsem.at[offset],
-            {"mem": lax.rem(me + offset, PARTS)},
-        )
-
-    def pred_copy(offset):
-        other = lax.rem(me + offset, PARTS)
-        return remote(
-            pred_send.at[other], pred_recv.at[me], pred_ssem.at[offset], pred_rsem.at[offset],
-            {"mem": other},
-        )
-
-    def cell_copy(chunk, offset):
-        other = lax.rem(me + offset, PARTS)
-        return remote(
-            cell_send.at[other, chunk], cell_recv.at[chunk, me],
-            cell_ssem.at[chunk, offset], cell_rsem.at[chunk, offset], {"mem": other},
-        )
-
-    def back_copy(chunk, offset):
-        other = lax.rem(me + offset, PARTS)
-        return remote(
-            back_send.at[chunk, other], back_recv.at[chunk, me],
-            back_ssem.at[chunk, offset], back_rsem.at[chunk, offset], {"mem": other},
-        )
-
-    def each(action):
-        def step(offset, carry):
-            action(offset)
-            return carry
-
-        lax.fori_loop(1, PARTS, step, 0)
-
-    to_right = remote(down_send, top_halo, halo_ssem.at[0], halo_rsem.at[0], {"tile": right})
-    to_left = remote(up_send, low_halo, halo_ssem.at[1], halo_rsem.at[1], {"tile": left})
-    to_right.start()
-    to_left.start()
-    for load in loads[3:]:
-        load.wait()
-    each(lambda offset: oc_copy(offset).start())
-    oc[me] = cells_ref[0]
-
 
     def inner_send(low, number, carry):
         turned = lax.rem(number + lax.div(me + 1, 2), PARTS // 2)
         part = 4 * lax.div(turned, 2) + 1 + lax.rem(turned, 2)
         offset = lax.rem(part - me + PARTS, PARTS)
 
-        @pl.when(offset > 0)
+        @pl.when((offset > 0) & (lax.div(part, 2) <= plane))
         def _():
             for chunk in range(CHUNKS):
                 remote(
@@ -262,6 +282,20 @@
     lax.fori_loop(half_count // 2, LOCAL // 2, inner_pair, 0)
     lax.fori_loop(0, PARTS // 2, functools.partial(inner_cells, half_count), 0)
     lax.fori_loop(0, PARTS // 2, functools.partial(inner_send, half_count), 0)
+
+    def later(number, carry):
+        @pl.when(number > plane)
+        def _():
+            pl.semaphore_wait(ready.at[number], 2)
+            for part in (2 * number, 2 * number + 1):
+                oc_copy(lax.rem(part - me + PARTS, PARTS)).start()
+            part = 2 * number + 1 - lax.rem(number, 2)
+            for chunk in range(CHUNKS):
+                cell_copy(chunk, lax.rem(part - me + PARTS, PARTS)).start()
+
+        return carry
+
+    lax.fori_loop(1, PARTS // 2, later, 0)
 
     each(lambda offset: oc_copy(offset).wait())
     within = lax.broadcasted_iota(jnp.int32, (WIDE, NOBS), 0)
@@ -528,6 +562,7 @@
             pltpu.VMEM((MEMBERS, 1), F32),
             pltpu.VMEM((CHUNKS, PARTS, LOCAL, WIDE), BF16),
             pltpu.VMEM((CHUNKS, PARTS, LOCAL, WIDE), BF16),
+            pltpu.SemaphoreType.REGULAR((PARTS // 2,)),
             dma((6,)), dma((2,)), dma((2,)),
             dma((PARTS,)), dma((PARTS,)), dma((PARTS,)), dma((PARTS,)),
             dma((CHUNKS, PARTS)), dma((CHUNKS, PARTS)),

time: 79.2 us -> 88.4 us (1.12)
  Pallas kernels: 77.7 us -> 86.9 us
    pallas_call x1, Pallas kernels: 77.7 us -> 86.9 us  [on_device(): pl.pallas_call(kernel, name='cycle', out_shape=pltpu.VMEM(ensemble.shape,...]
where the time goes in v4:
time: 88.4 us; the launch traced here: 88.2 us
  Pallas kernels  86.9 us (98%)
  local copies, waits for them, and re-layouts  1.32 us (1%)
    pallas_call x1, Pallas kernels, on_device(): pl.pallas_call(kernel, name='cycle', out_shape=pltpu.VMEM(ensemble.shape,...  86.9 us

profile of v4, /device:TPU:1, one launch (start us, length us, event | category | flops | bytes accessed | tf_op | source)
XLA Modules:
  0.0 88.2 jit_solution(10974395167947237242)
XLA Ops:
  0.0 86.9 %cycle.1 = f32[32,4,32,128]{3,2,1,0:T(8,128)S(1)} custom-call(f32[32,4,32,128]{3,2,1,0:T(8,128)} %ens_hbm.1, f32[4,32,128]{2,1,0:T(8,128)} %dif_hbm.1, s32[1,1,512]{2,1,0:T(1,128)} %cells_hbm.1, f32[1,1,512]{2,1,0:T(1,128)} %values_hbm.1, f32[1,1,512]{2,1,0:T(1,128)} %weights_hbm.1), custom_call_target="tpu_custom_call" | custom-call | tf_op jit(solution)/shard_map/cycle/pallas_call | solution.py:537
  86.9 1.3 %copy.7 = f32[32,4,32,128]{3,2,1,0:T(8,128)} copy(f32[32,4,32,128]{3,2,1,0:T(8,128)S(1)} %cycle.1) | data formatting | bytes 4194304

commit v5 on v3

--- a/solution.py
+++ b/solution.py
@@ -105,6 +105,17 @@
     tiles = lax.axis_size("tile")
     right, left = lax.rem(tile + 1, tiles), lax.rem(tile + tiles - 1, tiles)
 
+    def order(number):
+        half = lax.div(number + 1, 2)
+        return jnp.where(lax.rem(number, 2) == 0, PARTS // 2 + half, PARTS // 2 - half)
+
+    def each(action):
+        def step(number, carry):
+            action(order(number))
+            return carry
+
+        lax.fori_loop(0, PARTS - 1, step, 0)
+
     half_count = LOCAL // 2
     loads = [
         pltpu.make_async_copy(source, target, load_sem.at[number])
@@ -122,10 +133,11 @@
     for load in loads:
         load.start()
     barrier = pltpu.get_barrier_semaphore()
-    for offset in range(1, PARTS):
-        pl.semaphore_signal(
+    each(
+        lambda offset: pl.semaphore_signal(
             barrier, inc=1, device_id={"mem": lax.rem(me + offset, PARTS)}, device_id_type=MESH
         )
+    )
     for other in (left, right):
         pl.semaphore_signal(barrier, inc=1, device_id={"tile": other}, device_id_type=MESH)
     loads[0].wait()
@@ -225,13 +237,6 @@
             back_ssem.at[chunk, offset], back_rsem.at[chunk, offset], {"mem": other},
         )
 
-    def each(action):
-        def step(offset, carry):
-            action(offset)
-            return carry
-
-        lax.fori_loop(1, PARTS, step, 0)
-
     to_right = remote(down_send, top_halo, halo_ssem.at[0], halo_rsem.at[0], {"tile": right})
     to_left = remote(up_send, low_halo, halo_ssem.at[1], halo_rsem.at[1], {"tile": left})
     to_right.start()
@@ -242,12 +247,13 @@
     oc[me] = cells_ref[0]
 
 
-    def inner_send(low, number, carry):
-        turned = lax.rem(number + lax.div(me + 1, 2), PARTS // 2)
-        part = 4 * lax.div(turned, 2) + 1 + lax.rem(turned, 2)
-        offset = lax.rem(part - me + PARTS, PARTS)
-
-        @pl.when(offset > 0)
+    def inner(part):
+        return lax.rem(lax.rem(part, 4) + 1, 4) >= 2
+
+    def inner_send(low, offset):
+        part = lax.rem(me + offset, PARTS)
+
+        @pl.when(inner(part))
         def _():
             for chunk in range(CHUNKS):
                 remote(
@@ -256,12 +262,10 @@
                     cell_ssem.at[chunk, offset], cell_rsem.at[chunk, offset], {"mem": part},
                 ).start()
 
-        return carry
-
-    lax.fori_loop(0, PARTS // 2, functools.partial(inner_send, 0), 0)
+    each(functools.partial(inner_send, 0))
     lax.fori_loop(half_count // 2, LOCAL // 2, inner_pair, 0)
     lax.fori_loop(0, PARTS // 2, functools.partial(inner_cells, half_count), 0)
-    lax.fori_loop(0, PARTS // 2, functools.partial(inner_send, half_count), 0)
+    each(functools.partial(inner_send, half_count))
 
     each(lambda offset: oc_copy(offset).wait())
     within = lax.broadcasted_iota(jnp.int32, (WIDE, NOBS), 0)
@@ -357,10 +361,6 @@
 
     lax.fori_loop(0, PARTS // 2, edge_cells, 0)
 
-    def order(number):
-        half = lax.div(number + 1, 2)
-        return jnp.where(lax.rem(number, 2) == 0, PARTS // 2 + half, PARTS // 2 - half)
-
     def gather(number, carry):
         part = lax.rem(me + order(number), PARTS)
         group = jnp.broadcast_to(jnp.right_shift(oc[part], 8), (LOCAL, NOBS))
@@ -381,14 +381,11 @@
 
     lax.fori_loop(0, PARTS, gather, 0)
     for chunk in range(CHUNKS):
-        def edge_send(number, carry):
-            turned = lax.rem(number + lax.div(me + 1, 2), PARTS // 2)
-            part = 4 * lax.div(turned, 2) + 3 * lax.rem(turned, 2)
-            offset = lax.rem(part - me + PARTS, PARTS)
-            pl.when(offset > 0)(lambda: cell_copy(chunk, offset).start())
-            return carry
-
-        lax.fori_loop(0, PARTS // 2, edge_send, 0)
+        def edge_send(offset):
+            part = lax.rem(me + offset, PARTS)
+            pl.when(jnp.logical_not(inner(part)))(lambda: cell_copy(chunk, offset).start())
+
+        each(edge_send)
         cell_recv[chunk, me] = cell_send[me, chunk]
     pred_recv[me] = pred_send[me]
 

time: 79.2 us -> 79.6 us (level)
  no operation moved by 1% of the time
where the time goes in v5:
time: 79.6 us; the launch traced here: 79.5 us
  Pallas kernels  78.2 us (98%)
  local copies, waits for them, and re-layouts  1.32 us (2%)
    pallas_call x1, Pallas kernels, on_device(): pl.pallas_call(kernel, name='cycle', out_shape=pltpu.VMEM(ensemble.shape,...  78.2 us

profile of v5, /device:TPU:1, one launch (start us, length us, event | category | flops | bytes accessed | tf_op | source)
XLA Modules:
  0.0 79.5 jit_solution(780999887809417541)
XLA Ops:
  0.0 78.2 %cycle.1 = f32[32,4,32,128]{3,2,1,0:T(8,128)S(1)} custom-call(f32[32,4,32,128]{3,2,1,0:T(8,128)} %ens_hbm.1, f32[4,32,128]{2,1,0:T(8,128)} %dif_hbm.1, s32[1,1,512]{2,1,0:T(1,128)} %cells_hbm.1, f32[1,1,512]{2,1,0:T(1,128)} %values_hbm.1, f32[1,1,512]{2,1,0:T(1,128)} %weights_hbm.1), custom_call_target="tpu_custom_call" | custom-call | tf_op jit(solution)/shard_map/cycle/pallas_call | solution.py:500
  78.2 1.3 %copy.7 = f32[32,4,32,128]{3,2,1,0:T(8,128)} copy(f32[32,4,32,128]{3,2,1,0:T(8,128)S(1)} %cycle.1) | data formatting | bytes 4194304

commit v6 on v5

--- a/solution.py
+++ b/solution.py
@@ -18,8 +18,10 @@
 LANES = 128
 MEMBERS = 512
 NOBS = 512
-CHUNKS = 4
-WIDE = 256
+CHUNKS = 2
+WIDE = 512
+SPAN = WIDE // LANES
+HOT = 256
 PITCH = 40
 MESH = pl.DeviceIdType.MESH
 F32 = jnp.float32
@@ -167,8 +169,8 @@
 
     def to_cells(part, low, count):
         for chunk in range(CHUNKS):
-            for half in range(2):
-                first = pl.multiple_of((part * 8 + 2 * chunk + half) * PITCH + low, 8)
+            for half in range(SPAN):
+                first = pl.multiple_of((part * 8 + SPAN * chunk + half) * PITCH + low, 8)
                 cell_send[part, chunk, low : low + count, half * LANES : (half + 1) * LANES] = (
                     turn[pl.ds(first, count), :].astype(BF16)
                 )
@@ -268,10 +270,10 @@
     each(functools.partial(inner_send, half_count))
 
     each(lambda offset: oc_copy(offset).wait())
-    within = lax.broadcasted_iota(jnp.int32, (WIDE, NOBS), 0)
+    within = lax.broadcasted_iota(jnp.int32, (HOT, NOBS), 0)
 
     def mark(part, carry):
-        index = jnp.bitwise_and(oc[part], WIDE - 1)
+        index = jnp.bitwise_and(oc[part], HOT - 1)
         hot[part] = jnp.where(within == index, 1.0, 0.0).astype(BF16)
         return carry
 
@@ -368,10 +370,11 @@
         for step in (PARTS - 1, 0, 1):
             other = lax.rem(part + step, PARTS)
             for chunk in range(CHUNKS):
-                pieces.append(cell_send[other, chunk])
+                for first in range(0, WIDE, HOT):
+                    pieces.append(cell_send[other, chunk, :, first : first + HOT])
         found = jnp.dot(jnp.concatenate(pieces, axis=0), hot[part], preferred_element_type=F32)
         total = jnp.zeros((LOCAL, NOBS), F32)
-        for piece in range(3 * CHUNKS):
+        for piece in range(3 * CHUNKS * (WIDE // HOT)):
             total += jnp.where(
                 group == piece, found[LOCAL * piece : LOCAL * piece + LOCAL], 0.0
             )
@@ -473,8 +476,8 @@
         each(lambda offset: back_copy(chunk, offset).wait())
 
         def from_cells(part, carry):
-            for half in range(2):
-                first = pl.multiple_of((part * 8 + 2 * chunk + half) * PITCH, 8)
+            for half in range(SPAN):
+                first = pl.multiple_of((part * 8 + SPAN * chunk + half) * PITCH, 8)
                 turn[pl.ds(first, LOCAL), :] = back_recv[
                     chunk, part, :, half * LANES : (half + 1) * LANES
                 ].astype(F32)
@@ -515,7 +518,7 @@
             pltpu.VMEM((LEVELS, 16, LANES), F32),
             pltpu.VMEM((LEVELS * ROWS * PITCH, LANES), F32),
             pltpu.VMEM((PARTS, 1, NOBS), jnp.int32),
-            pltpu.VMEM((PARTS, WIDE, NOBS), BF16),
+            pltpu.VMEM((PARTS, HOT, NOBS), BF16),
             pltpu.VMEM((PARTS, CHUNKS, LOCAL, WIDE), BF16),
             pltpu.VMEM((CHUNKS, PARTS, LOCAL, WIDE), BF16),
             pltpu.VMEM((PARTS, LOCAL, NOBS), BF16),

time: 79.6 us -> 78.5 us (0.986)
  Pallas kernels: 78.2 us -> 77 us
    pallas_call x1, Pallas kernels: 78.2 us -> 77 us  [on_device(): pl.pallas_call(kernel, name='cycle', out_shape=pltpu.VMEM(ensemble.shape,...]
where the time goes in v6:
time: 78.5 us; the launch traced here: 78.3 us
  Pallas kernels  77 us (98%)
  local copies, waits for them, and re-layouts  1.32 us (2%)
    pallas_call x1, Pallas kernels, on_device(): pl.pallas_call(kernel, name='cycle', out_shape=pltpu.VMEM(ensemble.shape,...  77 us

profile of v6, /device:TPU:1, one launch (start us, length us, event | category | flops | bytes accessed | tf_op | source)
XLA Modules:
  0.0 78.3 jit_solution(2040241696949853501)
XLA Ops:
  0.0 77.0 %cycle.1 = f32[32,4,32,128]{3,2,1,0:T(8,128)S(1)} custom-call(f32[32,4,32,128]{3,2,1,0:T(8,128)} %ens_hbm.1, f32[4,32,128]{2,1,0:T(8,128)} %dif_hbm.1, s32[1,1,512]{2,1,0:T(1,128)} %cells_hbm.1, f32[1,1,512]{2,1,0:T(1,128)} %values_hbm.1, f32[1,1,512]{2,1,0:T(1,128)} %weights_hbm.1), custom_call_target="tpu_custom_call" | custom-call | tf_op jit(solution)/shard_map/cycle/pallas_call | solution.py:503
  77.0 1.3 %copy.7 = f32[32,4,32,128]{3,2,1,0:T(8,128)} copy(f32[32,4,32,128]{3,2,1,0:T(8,128)S(1)} %cycle.1) | data formatting | bytes 4194304

commit v7 on v6

--- a/solution.py
+++ b/solution.py
@@ -18,6 +18,7 @@
 LANES = 128
 MEMBERS = 512
 NOBS = 512
+PATCH = 1024
 CHUNKS = 2
 WIDE = 512
 SPAN = WIDE // LANES
@@ -97,9 +98,9 @@
 def kernel(
     ens_hbm, dif_hbm, cells_hbm, values_hbm, weights_hbm, out_ref,
     ens, dif_ref, cells_ref, values_ref, weights_ref, up_send, down_send, top_halo, low_halo, coef, edge_coef, edge_dif, turn,
-    oc, hot, cell_send, cell_recv, pred_send, pred_recv,
+    oc, hot, hot_own, near, near_recv, cell_send, cell_recv, pred_send, pred_recv,
     ymat, zmat, mmat, root, drive, back_send, back_recv,
-    load_sem, halo_ssem, halo_rsem, oc_ssem, oc_rsem, pred_ssem, pred_rsem,
+    load_sem, halo_ssem, halo_rsem, oc_ssem, oc_rsem, pred_ssem, pred_rsem, near_ssem, near_rsem,
     cell_ssem, cell_rsem, back_ssem, back_rsem,
 ):
     me = lax.axis_index("mem")
@@ -221,15 +222,17 @@
     def pred_copy(offset):
         other = lax.rem(me + offset, PARTS)
         return remote(
-            pred_send.at[other], pred_recv.at[me], pred_ssem.at[offset], pred_rsem.at[offset],
+            pred_send.at[other], pred_recv.at[me, pl.ds(half_count, half_count)], pred_ssem.at[offset], pred_rsem.at[offset],
             {"mem": other},
         )
 
-    def cell_copy(chunk, offset):
+    def cell_copy(side, chunk, offset):
         other = lax.rem(me + offset, PARTS)
+        rows = pl.ds(side * half_count, half_count)
         return remote(
-            cell_send.at[other, chunk], cell_recv.at[chunk, me],
-            cell_ssem.at[chunk, offset], cell_rsem.at[chunk, offset], {"mem": other},
+            cell_send.at[other, chunk, rows], cell_recv.at[chunk, me, rows],
+            cell_ssem.at[side, chunk, offset], cell_rsem.at[side, chunk, offset],
+            {"mem": other},
         )
 
     def back_copy(chunk, offset):
@@ -252,22 +255,16 @@
     def inner(part):
         return lax.rem(lax.rem(part, 4) + 1, 4) >= 2
 
-    def inner_send(low, offset):
-        part = lax.rem(me + offset, PARTS)
-
-        @pl.when(inner(part))
+    def send(wanted, side, offset):
+        @pl.when(inner(lax.rem(me + offset, PARTS)) == wanted)
         def _():
             for chunk in range(CHUNKS):
-                remote(
-                    cell_send.at[part, chunk, pl.ds(low, half_count)],
-                    cell_recv.at[chunk, me, pl.ds(low, half_count)],
-                    cell_ssem.at[chunk, offset], cell_rsem.at[chunk, offset], {"mem": part},
-                ).start()
-
-    each(functools.partial(inner_send, 0))
+                cell_copy(side, chunk, offset).start()
+
+    each(functools.partial(send, True, 0))
     lax.fori_loop(half_count // 2, LOCAL // 2, inner_pair, 0)
     lax.fori_loop(0, PARTS // 2, functools.partial(inner_cells, half_count), 0)
-    each(functools.partial(inner_send, half_count))
+    each(functools.partial(send, True, 1))
 
     each(lambda offset: oc_copy(offset).wait())
     within = lax.broadcasted_iota(jnp.int32, (HOT, NOBS), 0)
@@ -363,34 +360,71 @@
 
     lax.fori_loop(0, PARTS // 2, edge_cells, 0)
 
+    each(functools.partial(send, False, 0))
+
     def gather(number, carry):
         part = lax.rem(me + order(number), PARTS)
-        group = jnp.broadcast_to(jnp.right_shift(oc[part], 8), (LOCAL, NOBS))
+        group = jnp.broadcast_to(jnp.right_shift(oc[part], 8), (half_count, NOBS))
         pieces = []
         for step in (PARTS - 1, 0, 1):
             other = lax.rem(part + step, PARTS)
             for chunk in range(CHUNKS):
                 for first in range(0, WIDE, HOT):
-                    pieces.append(cell_send[other, chunk, :, first : first + HOT])
+                    pieces.append(cell_send[other, chunk, half_count:, first : first + HOT])
         found = jnp.dot(jnp.concatenate(pieces, axis=0), hot[part], preferred_element_type=F32)
-        total = jnp.zeros((LOCAL, NOBS), F32)
+        total = jnp.zeros((half_count, NOBS), F32)
         for piece in range(3 * CHUNKS * (WIDE // HOT)):
             total += jnp.where(
-                group == piece, found[LOCAL * piece : LOCAL * piece + LOCAL], 0.0
+                group == piece, found[half_count * piece : half_count * piece + half_count], 0.0
             )
         pred_send[part] = total.astype(BF16)
         pl.when(number > 0)(lambda: pred_copy(order(number - 1)).start())
         return carry
 
     lax.fori_loop(0, PARTS, gather, 0)
+    pred_recv[me, half_count:] = pred_send[me]
     for chunk in range(CHUNKS):
-        def edge_send(offset):
-            part = lax.rem(me + offset, PARTS)
-            pl.when(jnp.logical_not(inner(part)))(lambda: cell_copy(chunk, offset).start())
-
-        each(edge_send)
         cell_recv[chunk, me] = cell_send[me, chunk]
-    pred_recv[me] = pred_send[me]
+        each(lambda offset: cell_copy(0, chunk, offset).wait())
+
+    def find(step, carry):
+        index = oc[lax.rem(me + step + PARTS - 1, PARTS)] - PATCH * (2 - step)
+        for block in range(PATCH // HOT):
+            hot_own[HOT * block : HOT * block + HOT, :] = jnp.where(
+                within == index - HOT * block, 1.0, 0.0
+            ).astype(BF16)
+        found = jnp.zeros((half_count * PARTS, NOBS), F32)
+        for chunk in range(CHUNKS):
+            rows = [cell_recv[chunk, part, 0:half_count] for part in range(PARTS)]
+            found += jnp.dot(
+                jnp.concatenate(rows, axis=0),
+                hot_own[WIDE * chunk : WIDE * chunk + WIDE, :],
+                preferred_element_type=F32,
+            )
+        near[step] = found.astype(BF16)
+        return carry
+
+    lax.fori_loop(0, 3, find, 0)
+    to_last = remote(
+        near.at[0], near_recv.at[1], near_ssem.at[0], near_rsem.at[0],
+        {"mem": lax.rem(me + PARTS - 1, PARTS)},
+    )
+    to_next = remote(
+        near.at[2], near_recv.at[0], near_ssem.at[1], near_rsem.at[1],
+        {"mem": lax.rem(me + 1, PARTS)},
+    )
+    to_last.start()
+    to_next.start()
+    each(functools.partial(send, False, 1))
+    to_last.wait()
+    to_next.wait()
+    for part in range(PARTS):
+        rows = slice(half_count * part, half_count * part + half_count)
+        pred_recv[part, 0:half_count] = (
+            near[1, rows, :].astype(F32)
+            + near_recv[0, rows, :].astype(F32)
+            + near_recv[1, rows, :].astype(F32)
+        ).astype(BF16)
 
     each(lambda offset: pred_copy(offset).wait())
     weights, values = weights_ref[0], values_ref[0]
@@ -457,7 +491,7 @@
     ymat[...] = (root[...] + wmean).astype(BF16)
 
     for chunk in range(CHUNKS):
-        each(lambda offset: cell_copy(chunk, offset).wait())
+        each(lambda offset: cell_copy(1, chunk, offset).wait())
         total = jnp.zeros((1, WIDE), F32)
         for part in range(PARTS):
             total += jnp.sum(cell_recv[chunk, part].astype(F32), axis=0, keepdims=True)
@@ -519,9 +553,12 @@
             pltpu.VMEM((LEVELS * ROWS * PITCH, LANES), F32),
             pltpu.VMEM((PARTS, 1, NOBS), jnp.int32),
             pltpu.VMEM((PARTS, HOT, NOBS), BF16),
+            pltpu.VMEM((PATCH, NOBS), BF16),
+            pltpu.VMEM((3, MEMBERS // 2, NOBS), BF16),
+            pltpu.VMEM((2, MEMBERS // 2, NOBS), BF16),
             pltpu.VMEM((PARTS, CHUNKS, LOCAL, WIDE), BF16),
             pltpu.VMEM((CHUNKS, PARTS, LOCAL, WIDE), BF16),
-            pltpu.VMEM((PARTS, LOCAL, NOBS), BF16),
+            pltpu.VMEM((PARTS, LOCAL // 2, NOBS), BF16),
             pltpu.VMEM((PARTS, LOCAL, NOBS), BF16),
             square, square, square,
             pltpu.VMEM((MEMBERS, MEMBERS), F32),
@@ -530,7 +567,8 @@
             pltpu.VMEM((CHUNKS, PARTS, LOCAL, WIDE), BF16),
             dma((6,)), dma((2,)), dma((2,)),
             dma((PARTS,)), dma((PARTS,)), dma((PARTS,)), dma((PARTS,)),
-            dma((CHUNKS, PARTS)), dma((CHUNKS, PARTS)),
+            dma((2,)), dma((2,)),
+            dma((2, CHUNKS, PARTS)), dma((2, CHUNKS, PARTS)),
             dma((CHUNKS, PARTS)), dma((CHUNKS, PARTS)),
         ],
         compiler_params=pltpu.CompilerParams(

time: 78.5 us -> 80.9 us (1.031)
  Pallas kernels: 77 us -> 79.4 us
    pallas_call x1, Pallas kernels: 77 us -> 79.4 us  [on_device(): pl.pallas_call(kernel, name='cycle', out_shape=pltpu.VMEM(ensemble.shape,...]
where the time goes in v7:
time: 80.9 us; the launch traced here: 80.7 us
  Pallas kernels  79.4 us (98%)
  local copies, waits for them, and re-layouts  1.32 us (2%)
    pallas_call x1, Pallas kernels, on_device(): pl.pallas_call(kernel, name='cycle', out_shape=pltpu.VMEM(ensemble.shape,...  79.4 us

profile of v7, /device:TPU:1, one launch (start us, length us, event | category | flops | bytes accessed | tf_op | source)
XLA Modules:
  0.0 80.7 jit_solution(6523533539907346963)
XLA Ops:
  0.0 79.4 %cycle.1 = f32[32,4,32,128]{3,2,1,0:T(8,128)S(1)} custom-call(f32[32,4,32,128]{3,2,1,0:T(8,128)} %ens_hbm.1, f32[4,32,128]{2,1,0:T(8,128)} %dif_hbm.1, s32[1,1,512]{2,1,0:T(1,128)} %cells_hbm.1, f32[1,1,512]{2,1,0:T(1,128)} %values_hbm.1, f32[1,1,512]{2,1,0:T(1,128)} %weights_hbm.1), custom_call_target="tpu_custom_call" | custom-call | tf_op jit(solution)/shard_map/cycle/pallas_call | solution.py:537
  79.4 1.3 %copy.7 = f32[32,4,32,128]{3,2,1,0:T(8,128)} copy(f32[32,4,32,128]{3,2,1,0:T(8,128)S(1)} %cycle.1) | data formatting | bytes 4194304

commit v8 on v6

--- a/solution.py
+++ b/solution.py
@@ -167,8 +167,8 @@
                     ]
         return carry
 
-    def to_cells(part, low, count):
-        for chunk in range(CHUNKS):
+    def to_cells(part, low, count, chunks=range(CHUNKS)):
+        for chunk in chunks:
             for half in range(SPAN):
                 first = pl.multiple_of((part * 8 + SPAN * chunk + half) * PITCH + low, 8)
                 cell_send[part, chunk, low : low + count, half * LANES : (half + 1) * LANES] = (
@@ -191,18 +191,18 @@
                 tops.append(ens[2 * pair + half, level, 0:8, :])
                 lows.append(ens[2 * pair + half, level, ROWS - 8 : ROWS, :])
         for block, value in enumerate(pack(tops, 0)):
-            up_send[pair, 8 * block : 8 * block + 8, :] = value
+            up_send[pair + 1, 8 * block : 8 * block + 8, :] = value
         for block, value in enumerate(pack(lows, 5)):
-            down_send[pair, 8 * block : 8 * block + 8, :] = value
+            down_send[pair + 1, 8 * block : 8 * block + 8, :] = value
         return carry
 
     lax.fori_loop(0, LOCAL // 2, pack_pair, 0)
     tops = [dif_ref[level, 0:8, :] for level in range(LEVELS)]
     lows = [dif_ref[level, ROWS - 8 : ROWS, :] for level in range(LEVELS)]
     for block, value in enumerate(pack(tops, 0)):
-        up_send[LOCAL // 2, 8 * block : 8 * block + 8, :] = value
+        up_send[0, 8 * block : 8 * block + 8, :] = value
     for block, value in enumerate(pack(lows, 5)):
-        down_send[LOCAL // 2, 8 * block : 8 * block + 8, :] = value
+        down_send[0, 8 * block : 8 * block + 8, :] = value
 
     pl.semaphore_wait(barrier, PARTS + 1)
 
@@ -239,10 +239,22 @@
             back_ssem.at[chunk, offset], back_rsem.at[chunk, offset], {"mem": other},
         )
 
-    to_right = remote(down_send, top_halo, halo_ssem.at[0], halo_rsem.at[0], {"tile": right})
-    to_left = remote(up_send, low_halo, halo_ssem.at[1], halo_rsem.at[1], {"tile": left})
-    to_right.start()
-    to_left.start()
+    halos = []
+    for number, rows in enumerate((pl.ds(0, LOCAL // 4 + 1), pl.ds(LOCAL // 4 + 1, LOCAL // 4))):
+        halos.append(
+            [
+                remote(
+                    down_send.at[rows], top_halo.at[rows],
+                    halo_ssem.at[number, 0], halo_rsem.at[number, 0], {"tile": right},
+                ),
+                remote(
+                    up_send.at[rows], low_halo.at[rows],
+                    halo_ssem.at[number, 1], halo_rsem.at[number, 1], {"tile": left},
+                ),
+            ]
+        )
+        for copy in halos[number]:
+            copy.start()
     for load in loads[3:]:
         load.wait()
     each(lambda offset: oc_copy(offset).start())
@@ -269,6 +281,18 @@
     lax.fori_loop(0, PARTS // 2, functools.partial(inner_cells, half_count), 0)
     each(functools.partial(inner_send, half_count))
 
+    def upper_cells(level, carry):
+        to_cells(4 * level, 0, LOCAL, range(1, CHUNKS))
+        return carry
+
+    lax.fori_loop(0, LEVELS, upper_cells, 0)
+
+    def upper_send(offset):
+        first = lax.rem(lax.rem(me + offset, PARTS), 4) == 0
+        pl.when(first)(lambda: cell_copy(1, offset).start())
+
+    each(upper_send)
+
     each(lambda offset: oc_copy(offset).wait())
     within = lax.broadcasted_iota(jnp.int32, (HOT, NOBS), 0)
 
@@ -281,10 +305,10 @@
 
     top_mask = jnp.where(tile > 0, 1.0, 0.0).astype(F32)
     low_mask = jnp.where(tile < tiles - 1, 1.0, 0.0).astype(F32)
-    to_right.wait()
-    to_left.wait()
+    for copy in halos[0]:
+        copy.wait()
     extra = [
-        [halo[LOCAL // 2, 8 * block : 8 * block + 8, :] for block in range(3)]
+        [halo[0, 8 * block : 8 * block + 8, :] for block in range(3)]
         for halo in (top_halo, low_halo)
     ]
     for level in range(LEVELS):
@@ -315,8 +339,8 @@
         states, wests, easts = {}, {}, {}
         for number in members:
             pair, half = 2 * group + number // 2, number % 2
-            above = [top_halo[pair, 8 * n : 8 * n + 8, :] for n in range(3)]
-            below = [low_halo[pair, 8 * n : 8 * n + 8, :] for n in range(3)]
+            above = [top_halo[pair + 1, 8 * n : 8 * n + 8, :] for n in range(3)]
+            below = [low_halo[pair + 1, 8 * n : 8 * n + 8, :] for n in range(3)]
             for level in range(LEVELS):
                 at = 3 * (LEVELS * half + level)
                 block = (2 * pair + half, level)
@@ -355,13 +379,17 @@
                 turn[pl.ds(first + (ROWS - 3) * PITCH, 3, stride=PITCH), :] = value[11:14]
         return carry
 
-    lax.fori_loop(0, LOCAL // 4, edge_group, 0)
-
-    def edge_cells(number, carry):
-        to_cells(4 * (number // 2) + 3 * lax.rem(number, 2), 0, LOCAL)
-        return carry
-
-    lax.fori_loop(0, PARTS // 2, edge_cells, 0)
+    lax.fori_loop(0, LOCAL // 8, edge_group, 0)
+    for copy in halos[1]:
+        copy.wait()
+    lax.fori_loop(LOCAL // 8, LOCAL // 4, edge_group, 0)
+
+    def edge_cells(level, carry):
+        to_cells(4 * level, 0, LOCAL, range(1))
+        to_cells(4 * level + 3, 0, LOCAL)
+        return carry
+
+    lax.fori_loop(0, LEVELS, edge_cells, 0)
 
     def gather(number, carry):
         part = lax.rem(me + order(number), PARTS)
@@ -386,7 +414,8 @@
     for chunk in range(CHUNKS):
         def edge_send(offset):
             part = lax.rem(me + offset, PARTS)
-            pl.when(jnp.logical_not(inner(part)))(lambda: cell_copy(chunk, offset).start())
+            wanted = lax.rem(part, 4) == 3 if chunk else jnp.logical_not(inner(part))
+            pl.when(wanted)(lambda: cell_copy(chunk, offset).start())
 
         each(edge_send)
         cell_recv[chunk, me] = cell_send[me, chunk]
@@ -528,7 +557,7 @@
             pltpu.VMEM((MEMBERS, 1), F32),
             pltpu.VMEM((CHUNKS, PARTS, LOCAL, WIDE), BF16),
             pltpu.VMEM((CHUNKS, PARTS, LOCAL, WIDE), BF16),
-            dma((6,)), dma((2,)), dma((2,)),
+            dma((6,)), dma((2, 2)), dma((2, 2)),
             dma((PARTS,)), dma((PARTS,)), dma((PARTS,)), dma((PARTS,)),
             dma((CHUNKS, PARTS)), dma((CHUNKS, PARTS)),
             dma((CHUNKS, PARTS)), dma((CHUNKS, PARTS)),

time: 78.5 us -> 80.1 us (1.020)
  Pallas kernels: 77 us -> 78.6 us
    pallas_call x1, Pallas kernels: 77 us -> 78.6 us  [on_device(): pl.pallas_call(kernel, name='cycle', out_shape=pltpu.VMEM(ensemble.shape,...]
where the time goes in v8:
time: 80.1 us; the launch traced here: 80 us
  Pallas kernels  78.6 us (98%)
  local copies, waits for them, and re-layouts  1.32 us (2%)
    pallas_call x1, Pallas kernels, on_device(): pl.pallas_call(kernel, name='cycle', out_shape=pltpu.VMEM(ensemble.shape,...  78.6 us

profile of v8, /device:TPU:1, one launch (start us, length us, event | category | flops | bytes accessed | tf_op | source)
XLA Modules:
  0.0 80.0 jit_solution(339773843315694284)
XLA Ops:
  0.0 78.6 %cycle.1 = f32[32,4,32,128]{3,2,1,0:T(8,128)S(1)} custom-call(f32[32,4,32,128]{3,2,1,0:T(8,128)} %ens_hbm.1, f32[4,32,128]{2,1,0:T(8,128)} %dif_hbm.1, s32[1,1,512]{2,1,0:T(1,128)} %cells_hbm.1, f32[1,1,512]{2,1,0:T(1,128)} %values_hbm.1, f32[1,1,512]{2,1,0:T(1,128)} %weights_hbm.1), custom_call_target="tpu_custom_call" | custom-call | tf_op jit(solution)/shard_map/cycle/pallas_call | solution.py:532
  78.6 1.3 %copy.7 = f32[32,4,32,128]{3,2,1,0:T(8,128)} copy(f32[32,4,32,128]{3,2,1,0:T(8,128)S(1)} %cycle.1) | data formatting | bytes 4194304

commit v9 on v8

--- a/solution.py
+++ b/solution.py
@@ -167,8 +167,8 @@
                     ]
         return carry
 
-    def to_cells(part, low, count, chunks=range(CHUNKS)):
-        for chunk in chunks:
+    def to_cells(part, low, count):
+        for chunk in range(CHUNKS):
             for half in range(SPAN):
                 first = pl.multiple_of((part * 8 + SPAN * chunk + half) * PITCH + low, 8)
                 cell_send[part, chunk, low : low + count, half * LANES : (half + 1) * LANES] = (
@@ -280,18 +280,6 @@
     lax.fori_loop(half_count // 2, LOCAL // 2, inner_pair, 0)
     lax.fori_loop(0, PARTS // 2, functools.partial(inner_cells, half_count), 0)
     each(functools.partial(inner_send, half_count))
-
-    def upper_cells(level, carry):
-        to_cells(4 * level, 0, LOCAL, range(1, CHUNKS))
-        return carry
-
-    lax.fori_loop(0, LEVELS, upper_cells, 0)
-
-    def upper_send(offset):
-        first = lax.rem(lax.rem(me + offset, PARTS), 4) == 0
-        pl.when(first)(lambda: cell_copy(1, offset).start())
-
-    each(upper_send)
 
     each(lambda offset: oc_copy(offset).wait())
     within = lax.broadcasted_iota(jnp.int32, (HOT, NOBS), 0)
@@ -384,12 +372,11 @@
         copy.wait()
     lax.fori_loop(LOCAL // 8, LOCAL // 4, edge_group, 0)
 
-    def edge_cells(level, carry):
-        to_cells(4 * level, 0, LOCAL, range(1))
-        to_cells(4 * level + 3, 0, LOCAL)
-        return carry
-
-    lax.fori_loop(0, LEVELS, edge_cells, 0)
+    def edge_cells(number, carry):
+        to_cells(4 * (number // 2) + 3 * lax.rem(number, 2), 0, LOCAL)
+        return carry
+
+    lax.fori_loop(0, PARTS // 2, edge_cells, 0)
 
     def gather(number, carry):
         part = lax.rem(me + order(number), PARTS)
@@ -414,8 +401,7 @@
     for chunk in range(CHUNKS):
         def edge_send(offset):
             part = lax.rem(me + offset, PARTS)
-            wanted = lax.rem(part, 4) == 3 if chunk else jnp.logical_not(inner(part))
-            pl.when(wanted)(lambda: cell_copy(chunk, offset).start())
+            pl.when(jnp.logical_not(inner(part)))(lambda: cell_copy(chunk, offset).start())
 
         each(edge_send)
         cell_recv[chunk, me] = cell_send[me, chunk]

time: 80.1 us -> 77.8 us (0.971)
  Pallas kernels: 78.6 us -> 76.3 us
    pallas_call x1, Pallas kernels: 78.6 us -> 76.3 us  [on_device(): pl.pallas_call(kernel, name='cycle', out_shape=pltpu.VMEM(ensemble.shape,...]
where the time goes in v9:
time: 77.8 us; the launch traced here: 77.7 us
  Pallas kernels  76.3 us (98%)
  local copies, waits for them, and re-layouts  1.32 us (2%)
    pallas_call x1, Pallas kernels, on_device(): pl.pallas_call(kernel, name='cycle', out_shape=pltpu.VMEM(ensemble.shape,...  76.3 us

profile of v9, /device:TPU:1, one launch (start us, length us, event | category | flops | bytes accessed | tf_op | source)
XLA Modules:
  0.0 77.7 jit_solution(2914456730401310353)
XLA Ops:
  0.0 76.3 %cycle.1 = f32[32,4,32,128]{3,2,1,0:T(8,128)S(1)} custom-call(f32[32,4,32,128]{3,2,1,0:T(8,128)} %ens_hbm.1, f32[4,32,128]{2,1,0:T(8,128)} %dif_hbm.1, s32[1,1,512]{2,1,0:T(1,128)} %cells_hbm.1, f32[1,1,512]{2,1,0:T(1,128)} %values_hbm.1, f32[1,1,512]{2,1,0:T(1,128)} %weights_hbm.1), custom_call_target="tpu_custom_call" | custom-call | tf_op jit(solution)/shard_map/cycle/pallas_call | solution.py:518
  76.3 1.3 %copy.7 = f32[32,4,32,128]{3,2,1,0:T(8,128)} copy(f32[32,4,32,128]{3,2,1,0:T(8,128)S(1)} %cycle.1) | data formatting | bytes 4194304

commit v10 on v9

--- a/solution.py
+++ b/solution.py
@@ -180,8 +180,7 @@
         return carry
 
     loads[1].wait()
-    lax.fori_loop(0, half_count // 2, inner_pair, 0)
-    lax.fori_loop(0, PARTS // 2, functools.partial(inner_cells, 0), 0)
+    lax.fori_loop(0, half_count // 4, inner_pair, 0)
     loads[2].wait()
 
     def pack_pair(pair, carry):
@@ -240,7 +239,8 @@
         )
 
     halos = []
-    for number, rows in enumerate((pl.ds(0, LOCAL // 4 + 1), pl.ds(LOCAL // 4 + 1, LOCAL // 4))):
+    for number in range(4):
+        rows = pl.ds(4 * number + 1, 4) if number else pl.ds(0, 5)
         halos.append(
             [
                 remote(
@@ -276,6 +276,8 @@
                     cell_ssem.at[chunk, offset], cell_rsem.at[chunk, offset], {"mem": part},
                 ).start()
 
+    lax.fori_loop(half_count // 4, half_count // 2, inner_pair, 0)
+    lax.fori_loop(0, PARTS // 2, functools.partial(inner_cells, 0), 0)
     each(functools.partial(inner_send, 0))
     lax.fori_loop(half_count // 2, LOCAL // 2, inner_pair, 0)
     lax.fori_loop(0, PARTS // 2, functools.partial(inner_cells, half_count), 0)
@@ -367,10 +369,11 @@
                 turn[pl.ds(first + (ROWS - 3) * PITCH, 3, stride=PITCH), :] = value[11:14]
         return carry
 
-    lax.fori_loop(0, LOCAL // 8, edge_group, 0)
-    for copy in halos[1]:
-        copy.wait()
-    lax.fori_loop(LOCAL // 8, LOCAL // 4, edge_group, 0)
+    for number in range(4):
+        if number:
+            for copy in halos[number]:
+                copy.wait()
+        lax.fori_loop(2 * number, 2 * number + 2, edge_group, 0)
 
     def edge_cells(number, carry):
         to_cells(4 * (number // 2) + 3 * lax.rem(number, 2), 0, LOCAL)
@@ -543,7 +546,7 @@
             pltpu.VMEM((MEMBERS, 1), F32),
             pltpu.VMEM((CHUNKS, PARTS, LOCAL, WIDE), BF16),
             pltpu.VMEM((CHUNKS, PARTS, LOCAL, WIDE), BF16),
-            dma((6,)), dma((2, 2)), dma((2, 2)),
+            dma((6,)), dma((4, 2)), dma((4, 2)),
             dma((PARTS,)), dma((PARTS,)), dma((PARTS,)), dma((PARTS,)),
             dma((CHUNKS, PARTS)), dma((CHUNKS, PARTS)),
             dma((CHUNKS, PARTS)), dma((CHUNKS, PARTS)),

time: 77.8 us -> 79 us (1.015)
  Pallas kernels: 76.3 us -> 77.5 us
    pallas_call x1, Pallas kernels: 76.3 us -> 77.5 us  [on_device(): pl.pallas_call(kernel, name='cycle', out_shape=pltpu.VMEM(ensemble.shape,...]
where the time goes in v10:
time: 79 us; the launch traced here: 78.9 us
  Pallas kernels  77.5 us (98%)
  local copies, waits for them, and re-layouts  1.32 us (2%)
    pallas_call x1, Pallas kernels, on_device(): pl.pallas_call(kernel, name='cycle', out_shape=pltpu.VMEM(ensemble.shape,...  77.5 us

profile of v10, /device:TPU:1, one launch (start us, length us, event | category | flops | bytes accessed | tf_op | source)
XLA Modules:
  0.0 78.9 jit_solution(13770983776133817115)
XLA Ops:
  0.0 77.5 %cycle.1 = f32[32,4,32,128]{3,2,1,0:T(8,128)S(1)} custom-call(f32[32,4,32,128]{3,2,1,0:T(8,128)} %ens_hbm.1, f32[4,32,128]{2,1,0:T(8,128)} %dif_hbm.1, s32[1,1,512]{2,1,0:T(1,128)} %cells_hbm.1, f32[1,1,512]{2,1,0:T(1,128)} %values_hbm.1, f32[1,1,512]{2,1,0:T(1,128)} %weights_hbm.1), custom_call_target="tpu_custom_call" | custom-call | tf_op jit(solution)/shard_map/cycle/pallas_call | solution.py:521
  77.6 1.3 %copy.7 = f32[32,4,32,128]{3,2,1,0:T(8,128)} copy(f32[32,4,32,128]{3,2,1,0:T(8,128)S(1)} %cycle.1) | data formatting | bytes 4194304
